TPU v7x, 32 devices: a whole 2x2x4 slice. The times are simulated.
32 devices in a mesh: blocks: 16 (over z, y, x), cross: 2 (over core).
Axes of the slice: x: 2, y: 2, z: 4, core: 2. Of those that a mesh axis runs over, the one named last changes fastest.
Arguments:
- f_home: float32 [1024, 19, 512], P(('blocks', 'cross')), may hold values from -0.5 to 1.5
- levels: int32 [1024], P(('blocks', 'cross')), may hold values from 0 to 1, as said below
- plan: int32 [1024], P(('blocks', 'cross')), may hold values from 0 to 1023, as said below
Outputs:
- f_owner: float32 [1024, 19, 512], P(('blocks', 'cross'))
Inputs may be any that keep to these rules, and one draw needn't show every extreme that they name: `levels`: exactly a quarter of the patches, 8 times the number of devices, have level 1. plan is a permutation of the patch numbers. Of the patches in the slots of one device of f_home, at most 2 have owner slots on one device, and in every draw some device sends exactly 2 to one owner; every device's owner slots receive exactly 8 patches of level 1.
All inputs are finite; a program needn't handle non-finite values.
Results may differ from a plain program's by a relative error of at most 0.0001.
Values sent between devices are 32-bit elements; how exact they have to be, the bound alone decides.
No kernel may reach another device: no remote copies, remote signals or barrier semaphores. Data moves between devices by JAX's collectives and lax.ppermute only.
A program may use at most 256 MiB of HBM per device.

v0:
```python
import jax
import jax.numpy as jnp
from jax import lax
from jax.sharding import PartitionSpec as P

FLOW_PATCHES = 1
SPAN_PATCHES = 4
DEPTH_PATCHES = 8
EDGE = 8
STEPS = 2
CELLS = 512


VELOCITIES = (
    (0, 0, 0),
    (1, 0, 0),
    (-1, 0, 0),
    (0, 1, 0),
    (0, -1, 0),
    (0, 0, 1),
    (0, 0, -1),
    (1, 1, 0),
    (-1, -1, 0),
    (1, -1, 0),
    (-1, 1, 0),
    (1, 0, 1),
    (-1, 0, -1),
    (1, 0, -1),
    (-1, 0, 1),
    (0, 1, 1),
    (0, -1, -1),
    (0, 1, -1),
    (0, -1, 1),
)
WEIGHTS = (1.0 / 3.0,) + (1.0 / 18.0,) * 6 + (1.0 / 36.0,) * 12
FACE_SPEEDS = (
    (2, 8, 10, 12, 14),
    (1, 7, 9, 11, 13),
    (4, 8, 9, 16, 18),
    (3, 7, 10, 15, 17),
    (6, 12, 13, 16, 17),
    (5, 11, 14, 15, 18),
)
TAU_COARSE = 0.55
TAU_FINE = 2.0 * TAU_COARSE - 0.5
RESCALE = TAU_FINE / (2.0 * TAU_COARSE)
INFLOW = 0.08


def extended_2(cells, sides, width):
    for axis, dim in sides:
        count = lax.axis_size(axis)
        head = lax.slice_in_dim(cells, 0, width, axis=dim)
        tail = lax.slice_in_dim(cells, cells.shape[dim] - width, cells.shape[dim], axis=dim)
        cells = jnp.concatenate(
            [
                lax.ppermute(tail, axis, [(i, (i + 1) % count) for i in range(count)]),
                cells,
                lax.ppermute(head, axis, [((i + 1) % count, i) for i in range(count)]),
            ],
            axis=dim,
        )
    return cells


def moments(field):
    density = jnp.sum(field, axis=1)
    velocity = []
    for axis_id in range(3):
        forward = [speed for speed in range(19) if VELOCITIES[speed][axis_id] == 1]
        backward = [speed for speed in range(19) if VELOCITIES[speed][axis_id] == -1]
        velocity.append(
            (jnp.sum(field[:, forward], axis=1) - jnp.sum(field[:, backward], axis=1)) / density
        )
    return (density, velocity)


def equilibrium(density, velocity, speeds):
    speed_sq = velocity[0] * velocity[0] + velocity[1] * velocity[1] + velocity[2] * velocity[2]
    columns = []
    for speed in speeds:
        step_x, step_y, step_z = VELOCITIES[speed]
        along = step_x * velocity[0] + step_y * velocity[1] + step_z * velocity[2]
        columns.append(
            WEIGHTS[speed] * density * (1.0 + 3.0 * along + 4.5 * along * along - 1.5 * speed_sq)
        )
    return jnp.stack(columns, axis=1)


def collide(field, relax_rate):
    density, velocity = moments(field)
    balance = equilibrium(density, velocity, range(19))
    relaxed = field + relax_rate[:, None, None, None, None] * (balance - field)
    return (relaxed, balance, density, velocity)


def layer(field, face_id):
    picker = [slice(None)] * field.ndim
    picker[2 + face_id // 2] = 0 if face_id % 2 == 0 else field.shape[-1] - 1
    return field[tuple(picker)]


def face_payload(relaxed, balance, send_scale):
    eq_faces = jnp.stack(
        [layer(balance[:, list(FACE_SPEEDS[face_id])], face_id) for face_id in range(6)], axis=1
    )
    out_faces = jnp.stack(
        [layer(relaxed[:, list(FACE_SPEEDS[face_id])], face_id) for face_id in range(6)], axis=1
    )
    return (eq_faces, send_scale[:, None, None, None, None] * (out_faces - eq_faces))


def inflow_column(speeds):
    values = []
    for speed in speeds:
        along = VELOCITIES[speed][0] * INFLOW
        values.append(
            WEIGHTS[speed] * (1.0 + 3.0 * along + 4.5 * along * along - 1.5 * INFLOW * INFLOW)
        )
    return jnp.array(values, jnp.float32)


def framed(center, top_row, bottom_row, left_col, right_col):
    middle = jnp.concatenate([left_col[..., :, None], center, right_col[..., :, None]], axis=-1)
    corner = jnp.zeros(top_row.shape[:-1] + (1,), top_row.dtype)
    upper = jnp.concatenate([corner, top_row, corner], axis=-1)[..., None, :]
    lower = jnp.concatenate([corner, bottom_row, corner], axis=-1)[..., None, :]
    return jnp.concatenate([upper, middle, lower], axis=-2)


def bordered(center, left_col, right_col):
    return jnp.concatenate([left_col[..., None], center, right_col[..., None]], axis=-1)


def assemble(eq_ext, neq_ext, recv_scale, inflow_side, outflow_side):
    size_x, size_y, size_z = recv_scale.shape
    factor = recv_scale[:, :, :, None, None, None]

    def neighbour(shift_x, shift_y, shift_z, face_id):
        window = (
            slice(1 + shift_x, 1 + shift_x + size_x),
            slice(1 + shift_y, 1 + shift_y + size_y),
            slice(1 + shift_z, 1 + shift_z + size_z),
            face_id,
        )
        return eq_ext[window] + factor * neq_ext[window]

    plane_west = framed(
        neighbour(-1, 0, 0, 1),
        neighbour(-1, -1, 0, 1)[..., -1, :],
        neighbour(-1, 1, 0, 1)[..., 0, :],
        neighbour(-1, 0, -1, 1)[..., :, -1],
        neighbour(-1, 0, 1, 1)[..., :, 0],
    )
    plane_east = framed(
        neighbour(1, 0, 0, 0),
        neighbour(1, -1, 0, 0)[..., -1, :],
        neighbour(1, 1, 0, 0)[..., 0, :],
        neighbour(1, 0, -1, 0)[..., :, -1],
        neighbour(1, 0, 1, 0)[..., :, 0],
    )
    plane_south = bordered(
        neighbour(0, -1, 0, 3),
        neighbour(0, -1, -1, 3)[..., :, -1],
        neighbour(0, -1, 1, 3)[..., :, 0],
    )
    plane_north = bordered(
        neighbour(0, 1, 0, 2), neighbour(0, 1, -1, 2)[..., :, -1], neighbour(0, 1, 1, 2)[..., :, 0]
    )
    plane_below = neighbour(0, 0, -1, 5)
    plane_above = neighbour(0, 0, 1, 4)
    plane_west = jnp.where(
        inflow_side[:, None, None, None, None, None],
        inflow_column(FACE_SPEEDS[1])[:, None, None],
        plane_west,
    )
    plane_east = jnp.where(
        outflow_side[:, None, None, None, None, None],
        inflow_column(FACE_SPEEDS[0])[:, None, None],
        plane_east,
    )
    return (plane_west, plane_east, plane_south, plane_north, plane_below, plane_above)


def propagate(relaxed, planes):
    extent = relaxed.shape[-1]
    padded = jnp.pad(relaxed, ((0, 0), (0, 0), (1, 1), (1, 1), (1, 1)))
    plane_west, plane_east, plane_south, plane_north, plane_below, plane_above = planes
    for column, speed in enumerate(FACE_SPEEDS[1]):
        padded = padded.at[:, speed, 0, :, :].set(plane_west[:, column])
    for column, speed in enumerate(FACE_SPEEDS[0]):
        padded = padded.at[:, speed, extent + 1, :, :].set(plane_east[:, column])
    for column, speed in enumerate(FACE_SPEEDS[3]):
        padded = padded.at[:, speed, 1 : extent + 1, 0, :].set(plane_south[:, column])
    for column, speed in enumerate(FACE_SPEEDS[2]):
        padded = padded.at[:, speed, 1 : extent + 1, extent + 1, :].set(plane_north[:, column])
    for column, speed in enumerate(FACE_SPEEDS[5]):
        padded = padded.at[:, speed, 1 : extent + 1, 1 : extent + 1, 0].set(plane_below[:, column])
    for column, speed in enumerate(FACE_SPEEDS[4]):
        padded = padded.at[:, speed, 1 : extent + 1, 1 : extent + 1, extent + 1].set(
            plane_above[:, column]
        )
    shifted = []
    for speed in range(19):
        step_x, step_y, step_z = VELOCITIES[speed]
        shifted.append(
            padded[
                :,
                speed,
                1 - step_x : 1 - step_x + extent,
                1 - step_y : 1 - step_y + extent,
                1 - step_z : 1 - step_z + extent,
            ]
        )
    return jnp.stack(shifted, axis=1)


def wrap_axis(values, axis_id):
    length = values.shape[axis_id]
    return jnp.concatenate(
        [
            lax.slice_in_dim(values, length - 1, length, axis=axis_id),
            values,
            lax.slice_in_dim(values, 0, 1, axis=axis_id),
        ],
        axis=axis_id,
    )


def pair_slots(target_dev):
    patch_total = target_dev.shape[0]
    order = jnp.arange(patch_total, dtype=jnp.int32)
    earlier = (target_dev[:, None] == target_dev[None, :]) & (order[None, :] < order[:, None])
    return jnp.sum(earlier.astype(jnp.int32), axis=1)


def pack(payload, target_dev, pair_slot, devices, capacity):
    buffer = jnp.zeros((devices, capacity) + payload.shape[1:], payload.dtype)
    return buffer.at[target_dev, pair_slot].set(payload)


def migrate(populations, levels, plan, target_dev, pair_slot, devices, capacity):
    patch_total = populations.shape[0]
    metadata = jnp.stack([plan % patch_total + 1, levels], axis=1)
    recv_state, recv_meta = (
        lax.all_to_all(
            pack(populations, target_dev, pair_slot, devices, capacity),
            ("blocks", "cross"),
            split_axis=0,
            concat_axis=0,
            tiled=True,
        ),
        lax.all_to_all(
            pack(metadata, target_dev, pair_slot, devices, capacity),
            ("blocks", "cross"),
            split_axis=0,
            concat_axis=0,
            tiled=True,
        ),
    )
    total = devices * capacity
    flat_meta = recv_meta.reshape(total, 2)
    target = jnp.where(flat_meta[:, 0] > 0, flat_meta[:, 0] - 1, patch_total)
    anchor = jnp.arange(total, dtype=jnp.int32)
    moved = (
        jnp.zeros(populations.shape, populations.dtype)
        .at[target]
        .set(recv_state.reshape((total,) + populations.shape[1:]), mode="drop")
    )
    owner_levels = jnp.zeros((patch_total,), jnp.int32).at[target].set(flat_meta[:, 1], mode="drop")
    source_dev = (
        jnp.zeros((patch_total,), jnp.int32).at[target].set(anchor // capacity, mode="drop")
    )
    source_pair = (
        jnp.zeros((patch_total,), jnp.int32).at[target].set(anchor % capacity, mode="drop")
    )
    return (moved, owner_levels, source_dev, source_pair)


def home_ghosts(eq_faces, neq_faces, home_levels):
    lattice_shape = (FLOW_PATCHES, SPAN_PATCHES, DEPTH_PATCHES)
    patch_total = eq_faces.shape[0]
    stacked = jnp.stack([eq_faces, neq_faces], axis=1).reshape(lattice_shape + (-1,))
    extended = extended_2(stacked, (("blocks", 0), ("cross", 1)), 1)
    extended = wrap_axis(extended, 2)
    extended = extended.reshape(extended.shape[:3] + (2, 6, 5, EDGE, EDGE))
    recv_scale = (
        jnp.where(home_levels == 1, RESCALE, 1.0).astype(jnp.float32).reshape(lattice_shape)
    )
    span_x = FLOW_PATCHES * lax.axis_size("blocks")
    position = lax.axis_index("blocks") * FLOW_PATCHES + jnp.arange(FLOW_PATCHES, dtype=jnp.int32)
    planes = assemble(
        extended[:, :, :, 0],
        extended[:, :, :, 1],
        recv_scale,
        position == 0,
        position == span_x - 1,
    )
    return tuple((plane.reshape((patch_total,) + plane.shape[3:]) for plane in planes))


def body(f_home, levels, plan):
    devices = lax.axis_size(("blocks", "cross"))
    patch_total = f_home.shape[0]
    capacity = (patch_total + devices - 1) // devices + 1
    target_dev = plan // patch_total
    pair_slot = pair_slots(target_dev)
    send_home = jnp.where(levels == 1, 1.0 / RESCALE, 1.0).astype(jnp.float32)
    cube = (patch_total, 19, EDGE, EDGE, EDGE)
    populations = f_home.reshape(cube)
    fine_mask = levels == 1
    relax_rate = jnp.where(fine_mask, 1.0 / TAU_FINE, 1.0 / TAU_COARSE).astype(jnp.float32)
    fine_rate = jnp.full((patch_total,), 1.0 / TAU_FINE, jnp.float32)
    for round_id in range(STEPS):
        relaxed, balance, density, velocity = collide(populations, relax_rate)
        eq_faces, neq_faces = face_payload(relaxed, balance, send_home)
        planes = home_ghosts(eq_faces, neq_faces, levels)
        populations = propagate(relaxed, planes)
        updated = propagate(collide(populations, fine_rate)[0], planes)
        populations = jnp.where(fine_mask[:, None, None, None, None], updated, populations)
    return migrate(
        populations.reshape(patch_total, 19, CELLS),
        levels,
        plan,
        target_dev,
        pair_slot,
        devices,
        capacity,
    )[0]


def solution(mesh):
    in_specs = (P(("blocks", "cross"), None, None), P(("blocks", "cross")), P(("blocks", "cross")))
    out_specs = P(("blocks", "cross"), None, None)
    return jax.shard_map(body, mesh=mesh, in_specs=in_specs, out_specs=out_specs, check_vma=False)
```

profile of v0, /device:TPU:0, one launch (start us, length us, event | category | flops | bytes accessed | tf_op | source)
XLA Modules:
  0.0 1177.6 jit_solution(14872393180522574223)
XLA Ops:
  65.4 8.0 multiply_add_fusion.3
  104.0 5.2 reshape.9081
  109.3 5.6 copy.987
  122.2 16.7 %collective-permute-done = f32[1,4,8,3840]{3,2,1,0:T(8,128)S(1)} collective-permute-done((f32[1,4,8,3840]{3,2,1,0:T(8,128)S(1)}, f32[1,4,8,3840]{3,2,1,0:T(8,128)S(1)}, u32[]{:S(2)}, u32[]{:S(2)}) %collective-permute-start) | collective-permute-done | bytes 491552 | tf_op jit(solution)/shard_map/ppermute | solution.py:57
  141.5 10.2 pad.493
  156.7 27.5 %reshape.8613 = f32[3,6,10,2,6,5,8,8]{7,6,5,4,3,1,2,0:T(8,128)} reshape(f32[3,6,10,3840]{3,1,2,0:T(8,128)} %copy.787) | data formatting | bytes 5529600 | tf_op jit(solution)/shard_map/reshape | solution.py:286
  184.2 22.4 %slice_bitcast_fusion = (f32[3,6,10,6,5,8,8]{6,5,4,3,1,2,0:T(8,128)}, f32[3,6,10,1,6,5,8,8]{7,6,5,4,3,1,2,0:T(8,128)S(1)}) fusion(f32[3,6,10,2,6,5,8,8]{7,6,5,4,3,1,2,0:T(8,128)} %reshape.8613), kind=kLoop, calls=%fused_computation.51 | loop fusion | bytes 5529600 | tf_op jit(solution)/shard_map/squeeze | solution.py:294
  206.6 7.9 copy.1035
  214.5 8.3 fusion.345
  248.2 9.4 fusion.344
  283.7 6.4 slice_add_fusion.9
  290.2 11.0 copy.822
  436.9 7.7 pad.494
  495.2 5.9 fusion.340
  575.5 8.0 multiply_add_fusion.1
  613.4 5.2 reshape.9082
  618.6 5.7 copy.988
  630.0 17.1 %collective-permute-done.4 = f32[1,4,8,3840]{3,2,1,0:T(8,128)S(1)} collective-permute-done((f32[1,4,8,3840]{3,2,1,0:T(8,128)S(1)}, f32[1,4,8,3840]{3,2,1,0:T(8,128)S(1)}, u32[]{:S(2)}, u32[]{:S(2)}) %collective-permute-start.4) | collective-permute-done | bytes 491552 | tf_op jit(solution)/shard_map/ppermute | solution.py:57
  658.4 10.2 pad.495
  671.3 27.9 %reshape.9083 = f32[3,6,10,2,6,5,8,8]{7,6,5,4,3,2,1,0:T(8,128)} reshape(f32[3,6,10,3840]{3,2,1,0:T(8,128)} %fusion) | data formatting | bytes 5529600 | tf_op jit(solution)/shard_map/reshape | solution.py:286
  699.2 22.5 %fusion.341 = (f32[3,6,10,1,6,5,8,8]{7,6,5,4,3,2,1,0:T(8,128)}, f32[3,6,10,1,6,5,8,8]{7,6,5,4,3,2,1,0:T(8,128)S(1)}) fusion(f32[3,6,10,2,6,5,8,8]{7,6,5,4,3,2,1,0:T(8,128)} %reshape.9083), kind=kLoop, calls=%fused_computation.992 | loop fusion | bytes 5529600 | tf_op jit(solution)/shard_map/slice | solution.py:294
  721.7 7.9 copy.1034
  729.6 8.3 fusion.343
  741.7 17.2 %copy.1033 = f32[3,6,10,1,6,5,8,8]{7,6,5,1,2,4,0,3:T(8,128)} copy(f32[3,6,10,1,6,5,8,8]{7,6,5,4,3,2,1,0:T(8,128)} %get-tuple-element.1465) | data formatting | bytes 2764800
  758.9 9.3 fusion.342
  815.7 6.8 slice_add_fusion.1
  882.8 5.8 fusion.346
  996.3 7.7 pad.496
  1034.5 5.5 fusion.348
  1102.9 5.8 all-to-all-start.1
  1109.5 56.4 %all-to-all-done.1 = f32[32,2,19,512]{3,1,2,0:T(2,128)S(1)} async-done(((f32[32,2,19,512]{3,1,2,0:T(2,128)}), f32[32,2,19,512]{3,1,2,0:T(2,128)S(1)}, u32[]{:S(2)}, u32[]{:S(2)}) %all-to-all-start.1) | async-done | bytes 2490400 | tf_op jit(solution)/shard_map/all_to_all | solution.py:246
  1168.3 7.1 scatter_fusion.2
  (881 shorter events, 787.6 us)
Async XLA Ops:
  4.4 579.1 %copy-start.105 = (s32[1024]{0:T(1024)}, s32[1024]{0:T(1024)S(1)}, u32[]{:S(2)}) copy-start(s32[1024]{0:T(1024)S(1)} %get-tuple-element.1650) | copy-start | bytes 12292
  10.9 70.7 %copy-start.106 = (s32[1024]{0:T(1024)}, s32[1024]{0:T(1024)S(1)}, u32[]{:S(2)}) copy-start(s32[1024]{0:T(1024)S(1)} %get-tuple-element.1648) | copy-start | bytes 12292
  10.9 74.8 %copy-start.108 = (s32[1024]{0:T(1024)}, s32[1024]{0:T(1024)S(1)}, u32[]{:S(2)}) copy-start(s32[1024]{0:T(1024)S(1)} %get-tuple-element.1649) | copy-start | bytes 12292
  17.3 71.4 %copy-start.110 = (s32[1024]{0:T(1024)}, s32[1024]{0:T(1024)S(1)}, u32[]{:S(2)}) copy-start(s32[1024]{0:T(1024)S(1)} %get-tuple-element.1646) | copy-start | bytes 12292
  17.3 74.5 %copy-start.111 = (s32[1024]{0:T(1024)}, s32[1024]{0:T(1024)S(1)}, u32[]{:S(2)}) copy-start(s32[1024]{0:T(1024)S(1)} %get-tuple-element.1647) | copy-start | bytes 12292
  65.4 38.3 %copy-start.113 = (f32[32]{0:T(128)}, f32[32]{0:T(128)S(1)}, u32[]{:S(2)}) copy-start(f32[32]{0:T(128)S(1)} %get-tuple-element.1643) | copy-start | bytes 388
  65.4 86.3 %copy-start.112 = (f32[32]{0:T(128)}, f32[32]{0:T(128)S(1)}, u32[]{:S(2)}) copy-start(f32[32]{0:T(128)S(1)} %get-tuple-element.1641) | copy-start | bytes 388
  114.9 24.0 %collective-permute-start = (f32[1,4,8,3840]{3,2,1,0:T(8,128)S(1)}, f32[1,4,8,3840]{3,2,1,0:T(8,128)S(1)}, u32[]{:S(2)}, u32[]{:S(2)}) collective-permute-start(f32[1,4,8,3840]{3,2,1,0:T(8,128)S(1)} %copy.987), channel_id=1, source_target_pairs={{0,2},{2,4},{4,6},{6,8},{8,10},{10,12},{12,14},{14,16},{16,18},{18... | collective-permute-start | bytes 1474568 | tf_op jit(solution)/shard_map/ppermute | solution.py:57
  117.9 23.0 %collective-permute-start.1 = (f32[1,4,8,3840]{3,2,1,0:T(8,128)S(1)}, f32[1,4,8,3840]{3,2,1,0:T(8,128)S(1)}, u32[]{:S(2)}, u32[]{:S(2)}) collective-permute-start(f32[1,4,8,3840]{3,2,1,0:T(8,128)S(1)} %copy.987), channel_id=1, source_target_pairs={{2,0},{4,2},{6,4},{8,6},{10,8},{12,10},{14,12},{16,14},{18,16},{20... | collective-permute-start | bytes 1474568 | tf_op jit(solution)/shard_map/ppermute | solution.py:59
  140.9 11.5 collective-permute-start.2
  141.0 11.5 collective-permute-start.3
  151.9 163.6 %copy-start.87 = (f32[4,8]{0,1:T(8,128)}, f32[4,8]{0,1:T(8,128)S(1)}, u32[]{:S(2)}) copy-start(f32[4,8]{0,1:T(8,128)S(1)} %copy.789) | copy-start | bytes 388
  290.1 35.3 %copy-start.35 = (f32[32,5,8,8]{0,3,2,1:T(8,128)S(1)}, f32[32,5,8,8]{0,3,2,1:T(8,128)}, u32[]{:S(2)}) copy-start(f32[32,5,8,8]{0,3,2,1:T(8,128)} %squeeze.168) | copy-start | bytes 122884
  290.1 35.3 %copy-start.36 = (f32[32,5,8,8]{0,3,2,1:T(8,128)S(1)}, f32[32,5,8,8]{0,3,2,1:T(8,128)}, u32[]{:S(2)}) copy-start(f32[32,5,8,8]{0,3,2,1:T(8,128)} %squeeze.176) | copy-start | bytes 122884
  290.1 35.3 %copy-start.37 = (f32[32,5,8,8]{0,3,2,1:T(8,128)S(1)}, f32[32,5,8,8]{0,3,2,1:T(8,128)}, u32[]{:S(2)}) copy-start(f32[32,5,8,8]{0,3,2,1:T(8,128)} %squeeze.182) | copy-start | bytes 122884
  290.1 35.3 %copy-start.38 = (f32[32,5,8,8]{0,3,2,1:T(8,128)S(1)}, f32[32,5,8,8]{0,3,2,1:T(8,128)}, u32[]{:S(2)}) copy-start(f32[32,5,8,8]{0,3,2,1:T(8,128)} %squeeze.186) | copy-start | bytes 122884
  290.1 35.3 %copy-start.39 = (f32[32,5,8,8]{0,3,2,1:T(8,128)S(1)}, f32[32,5,8,8]{0,3,2,1:T(8,128)}, u32[]{:S(2)}) copy-start(f32[32,5,8,8]{0,3,2,1:T(8,128)} %squeeze.188) | copy-start | bytes 122884
  290.1 35.3 %copy-start.46 = (f32[32,5,8,8]{0,3,2,1:T(8,128)S(1)}, f32[32,5,8,8]{0,3,2,1:T(8,128)}, u32[]{:S(2)}) copy-start(f32[32,5,8,8]{0,3,2,1:T(8,128)} %squeeze.159) | copy-start | bytes 122884
  341.0 47.6 %copy-start.73 = (f32[32,1,8,8]{0,3,2,1:T(8,128)}, f32[32,1,8,8]{0,3,2,1:T(8,128)S(1)}, u32[]{:S(2)}) copy-start(f32[32,1,8,8]{0,3,2,1:T(8,128)S(1)} %get-tuple-element.1600) | copy-start | bytes 24580
  341.0 47.6 %copy-start.77 = (f32[32,1,8,8]{0,3,2,1:T(8,128)}, f32[32,1,8,8]{0,3,2,1:T(8,128)S(1)}, u32[]{:S(2)}) copy-start(f32[32,1,8,8]{0,3,2,1:T(8,128)S(1)} %get-tuple-element.1601) | copy-start | bytes 24580
  341.0 47.6 %copy-start.79 = (f32[32,1,8,8]{0,3,2,1:T(8,128)}, f32[32,1,8,8]{0,3,2,1:T(8,128)S(1)}, u32[]{:S(2)}) copy-start(f32[32,1,8,8]{0,3,2,1:T(8,128)S(1)} %get-tuple-element.1602) | copy-start | bytes 24580
  341.0 47.6 %copy-start.81 = (f32[32,1,8,8]{0,3,2,1:T(8,128)}, f32[32,1,8,8]{0,3,2,1:T(8,128)S(1)}, u32[]{:S(2)}) copy-start(f32[32,1,8,8]{0,3,2,1:T(8,128)S(1)} %get-tuple-element.1603) | copy-start | bytes 24580
  341.0 47.6 %copy-start.83 = (f32[32,1,8,8]{0,3,2,1:T(8,128)}, f32[32,1,8,8]{0,3,2,1:T(8,128)S(1)}, u32[]{:S(2)}) copy-start(f32[32,1,8,8]{0,3,2,1:T(8,128)S(1)} %get-tuple-element.1604) | copy-start | bytes 24580
  341.1 49.4 %copy-start.71 = (f32[32,1,8,8]{0,3,2,1:T(8,128)}, f32[32,1,8,8]{0,3,2,1:T(8,128)S(1)}, u32[]{:S(2)}) copy-start(f32[32,1,8,8]{0,3,2,1:T(8,128)S(1)} %get-tuple-element.1598) | copy-start | bytes 24580
  341.1 49.4 %copy-start.75 = (f32[32,1,8,8]{0,3,2,1:T(8,128)}, f32[32,1,8,8]{0,3,2,1:T(8,128)S(1)}, u32[]{:S(2)}) copy-start(f32[32,1,8,8]{0,3,2,1:T(8,128)S(1)} %get-tuple-element.1599) | copy-start | bytes 24580
  624.3 22.8 %collective-permute-start.4 = (f32[1,4,8,3840]{3,2,1,0:T(8,128)S(1)}, f32[1,4,8,3840]{3,2,1,0:T(8,128)S(1)}, u32[]{:S(2)}, u32[]{:S(2)}) collective-permute-start(f32[1,4,8,3840]{3,2,1,0:T(8,128)S(1)} %copy.988), channel_id=1, source_target_pairs={{0,2},{2,4},{4,6},{6,8},{8,10},{10,12},{12,14},{14,16},{16,18},{18... | collective-permute-start | bytes 1474568 | tf_op jit(solution)/shard_map/ppermute | solution.py:57
  625.8 23.7 %collective-permute-start.5 = (f32[1,4,8,3840]{3,2,1,0:T(8,128)S(1)}, f32[1,4,8,3840]{3,2,1,0:T(8,128)S(1)}, u32[]{:S(2)}, u32[]{:S(2)}) collective-permute-start(f32[1,4,8,3840]{3,2,1,0:T(8,128)S(1)} %copy.988), channel_id=1, source_target_pairs={{2,0},{4,2},{6,4},{8,6},{10,8},{12,10},{14,12},{16,14},{18,16},{20... | collective-permute-start | bytes 1474568 | tf_op jit(solution)/shard_map/ppermute | solution.py:59
  649.6 19.0 %collective-permute-start.6 = (f32[3,1,8,3840]{3,2,1,0:T(8,128)S(1)}, f32[3,1,8,3840]{3,2,1,0:T(8,128)S(1)}, u32[]{:S(2)}, u32[]{:S(2)}) collective-permute-start(f32[3,1,8,3840]{3,2,1,0:T(8,128)S(1)} %get-tuple-element.1581), channel_id=1, source_target_pairs={{0,1},{1,0},{2,3},{3,2},{4,5},{5,4},{6,7},{7,6},{8,9},{9,8},{10,11... | collective-permute-start | bytes 1105928 | tf_op jit(solution)/shard_map/ppermute | solution.py:57
  649.7 18.9 %collective-permute-start.7 = (f32[3,1,8,3840]{3,2,1,0:T(8,128)S(1)}, f32[3,1,8,3840]{3,2,1,0:T(8,128)S(1)}, u32[]{:S(2)}, u32[]{:S(2)}) collective-permute-start(f32[3,1,8,3840]{3,2,1,0:T(8,128)S(1)} %get-tuple-element.1582), channel_id=1, source_target_pairs={{1,0},{0,1},{3,2},{2,3},{5,4},{4,5},{7,6},{6,7},{9,8},{8,9},{11,10... | collective-permute-start | bytes 1105928 | tf_op jit(solution)/shard_map/ppermute | solution.py:59
  654.8 448.1 %all-to-all-start = ((s32[32,2,2]{2,1,0:T(2,128)}), s32[32,2,2]{2,1,0:T(2,128)}, u32[]{:S(2)}, u32[]{:S(2)}) async-start(s32[32,2,2]{2,1,0:T(2,128)} %scatter_fusion), calls=%async_computation | async-start | bytes 65536 | tf_op jit(solution)/shard_map/all_to_all | solution.py:253
  1044.9 47.6 %copy-start.118 = (pred[32]{0:T(512)(128)(4,1)S(1)}, pred[32]{0:T(512)(128)(4,1)}, u32[]{:S(2)}) copy-start(pred[32]{0:T(512)(128)(4,1)} %broadcast_compare_fusion) | copy-start | bytes 100
  1102.9 63.0 %all-to-all-start.1 = ((f32[32,2,19,512]{3,1,2,0:T(2,128)}), f32[32,2,19,512]{3,1,2,0:T(2,128)S(1)}, u32[]{:S(2)}, u32[]{:S(2)}) async-start(f32[32,2,19,512]{3,1,2,0:T(2,128)} %copy.982), calls=%async_computation.1 | async-start | bytes 4980736 | tf_op jit(solution)/shard_map/all_to_all | solution.py:246
  (106 other events, 1635.2 us)
where the time goes:
time: 1200 us; the launch traced here: 1180 us
  local copies, waits for them, and re-layouts  919 us (77%)
  other arithmetic  137 us (11%)
  waiting for transfers between devices  94.6 us (8%)
  starting transfers between devices  23.5 us (2%)
    unnamed x379, local copies, waits for them, and re-layouts  150 us
    slice x28, local copies, waits for them, and re-layouts, neighbour(): return eq_ext[window] + factor * neq_ext[window]  90 us
    another operation x43, local copies, waits for them, and re-layouts, propagate(): return jnp.stack(shifted, axis=1)  62.5 us
    all_to_all x1, waiting for transfers between devices, migrate(): lax.all_to_all(pack(populations, target_dev, pair_slot, devices, capacity...  56.4 us
    gather x23, local copies, waits for them, and re-layouts, face_payload(): balance[:, list(FACE_SPEEDS[face_id])]  55.4 us
    reshape x2, local copies, waits for them, and re-layouts, home_ghosts(): extended = extended.reshape(extended.shape[:3] + (2, 6, 5, EDGE, EDGE))  55.4 us
    squeeze x24, local copies, waits for them, and re-layouts, neighbour(): return eq_ext[window] + factor * neq_ext[window]  48.1 us
    unnamed x72, other arithmetic  47.8 us
  transfers between devices with their start and end apart: 10, of which 5 were waited for; matrix products, arithmetic and copies ran while one was open for 39% of the time, Pallas kernels for 0%

commit v1 on v0

v1 whole, which is shorter than its diff:
```python
import functools

import jax
import jax.numpy as jnp
from jax import lax
from jax.experimental import pallas as pl
from jax.experimental.pallas import tpu as pltpu
from jax.sharding import PartitionSpec as P

SPAN_PATCHES = 4
DEPTH_PATCHES = 8
EDGE = 8
STEPS = 2
CELLS = 512
LANES = 128
TILES = CELLS // LANES
ROWS = 80

VELOCITIES = (
    (0, 0, 0),
    (1, 0, 0),
    (-1, 0, 0),
    (0, 1, 0),
    (0, -1, 0),
    (0, 0, 1),
    (0, 0, -1),
    (1, 1, 0),
    (-1, -1, 0),
    (1, -1, 0),
    (-1, 1, 0),
    (1, 0, 1),
    (-1, 0, -1),
    (1, 0, -1),
    (-1, 0, 1),
    (0, 1, 1),
    (0, -1, -1),
    (0, 1, -1),
    (0, -1, 1),
)
SPEEDS = 19
WEIGHTS = (1.0 / 3.0,) + (1.0 / 18.0,) * 6 + (1.0 / 36.0,) * 12
EAST = (1, 7, 9, 11, 13)
WEST = (2, 8, 10, 12, 14)
NORTH = (3, 7, 10, 15, 17)
SOUTH = (4, 8, 9, 16, 18)
X_SPEEDS = EAST + WEST
Y_SPEEDS = NORTH + SOUTH
Y_PACKS = 3
DIAG_EAST = ((7, SPAN_PATCHES - 1), (9, 0))
DIAG_WEST = ((10, SPAN_PATCHES - 1), (8, 0))
TAU_COARSE = 0.55
TAU_FINE = 2.0 * TAU_COARSE - 0.5
RESCALE = TAU_FINE / (2.0 * TAU_COARSE)
INFLOW = 0.08


def inflow_value(speed):
    along = VELOCITIES[speed][0] * INFLOW
    return WEIGHTS[speed] * (1.0 + 3.0 * along + 4.5 * along * along - 1.5 * INFLOW * INFLOW)


def lane_roll(tile, shift):
    shift %= LANES
    return tile if shift == 0 else pltpu.roll(tile, shift, 1)


def equilibria(field):
    density = functools.reduce(lambda a, b: a + b, field)
    inverse = 1.0 / density
    velocity = []
    for axis_id in range(3):
        forward = [field[q] for q in range(SPEEDS) if VELOCITIES[q][axis_id] == 1]
        backward = [field[q] for q in range(SPEEDS) if VELOCITIES[q][axis_id] == -1]
        terms = [a - b for a, b in zip(forward, backward)]
        velocity.append(functools.reduce(lambda a, b: a + b, terms) * inverse)
    common = 1.0 - 1.5 * (
        velocity[0] * velocity[0] + velocity[1] * velocity[1] + velocity[2] * velocity[2]
    )
    scaled = {weight: weight * density for weight in set(WEIGHTS)}
    balance = [scaled[WEIGHTS[0]] * common]
    for q in range(1, SPEEDS, 2):
        along = None
        for component, speed in zip(VELOCITIES[q], velocity):
            if component == 0:
                continue
            if along is None:
                along = speed if component == 1 else -speed
            else:
                along = along + speed if component == 1 else along - speed
        even = common + 4.5 * (along * along)
        odd = 3.0 * along
        balance.append(scaled[WEIGHTS[q]] * (even + odd))
        balance.append(scaled[WEIGHTS[q]] * (even - odd))
    return balance


class Masks:
    def __init__(self):
        lane = lax.broadcasted_iota(jnp.int32, (8, LANES), 1)
        self.low = lane < 64
        self.high = lane >= 64
        span = (lane // 8) % 8
        depth = lane % 8
        self.span = span
        self.span_first = span == 0
        self.span_last = span == 7
        self.depth_first = depth == 0
        self.depth_last = depth == 7

    def leaving(self, speed, tile):
        step_x, step_y, step_z = VELOCITIES[speed]
        across_x = None
        if step_x == 1 and tile == TILES - 1:
            across_x = self.high
        if step_x == -1 and tile == 0:
            across_x = self.low
        across_y = {0: None, 1: self.span_last, -1: self.span_first}[step_y]
        across_z = {0: None, 1: self.depth_last, -1: self.depth_first}[step_z]
        return across_x, across_y, across_z

    def leaving_any(self, speed, tile):
        parts = [mask for mask in self.leaving(speed, tile) if mask is not None]
        return functools.reduce(jnp.logical_or, parts) if parts else None

    def shifted(self, tiles, speed):
        step_x, step_y, step_z = VELOCITIES[speed]
        if step_z:
            edge = self.depth_first if step_z == 1 else self.depth_last
            tiles = [
                jnp.where(edge, lane_roll(v, -7 * step_z), lane_roll(v, step_z)) for v in tiles
            ]
        if step_y:
            edge = self.span_first if step_y == 1 else self.span_last
            tiles = [
                jnp.where(edge, lane_roll(v, -56 * step_y), lane_roll(v, 8 * step_y)) for v in tiles
            ]
        if step_x:
            halves = [lane_roll(v, 64) for v in tiles]
            if step_x == 1:
                tiles = [
                    jnp.where(self.low, halves[t - 1], halves[t]) for t in range(TILES)
                ]
            else:
                tiles = [
                    jnp.where(self.low, halves[t], halves[(t + 1) % TILES]) for t in range(TILES)
                ]
        return tiles


def lanes_of(tile):
    return pl.ds(tile * LANES, LANES)


def emit_halos(masks, eq, neq, base, east_ref, west_ref, span_ref, diag_east_ref, diag_west_ref):
    last = TILES - 1

    def east_pack(speed, row):
        e = eq[speed, base + row, :, lanes_of(last)]
        n = neq[speed, base + row, :, lanes_of(last)]
        return jnp.where(masks.low, lane_roll(e, 64), n)

    def west_pack(speed, row):
        e = eq[speed, base + row, :, lanes_of(0)]
        n = neq[speed, base + row, :, lanes_of(0)]
        return jnp.where(masks.low, e, lane_roll(n, 64))

    for column in range(5):
        for row in range(SPAN_PATCHES):
            east_ref[column, row] = east_pack(EAST[column], row)
            west_ref[column, row] = west_pack(WEST[column], row)
    for column, (speed, row) in enumerate(DIAG_EAST):
        diag_east_ref[column] = east_pack(speed, row)
    for column, (speed, row) in enumerate(DIAG_WEST):
        diag_west_ref[column] = west_pack(speed, row)
    for pack_id in range(Y_PACKS):
        for tile in range(TILES):
            packed = jnp.zeros((8, LANES), jnp.float32)
            for slot in range(4):
                index = pack_id * 4 + slot
                if index >= len(Y_SPEEDS):
                    continue
                north = index < 5
                row = base + (SPAN_PATCHES - 1 if north else 0)
                at = 7 if north else 0
                e = eq[Y_SPEEDS[index], row, :, lanes_of(tile)]
                n = neq[Y_SPEEDS[index], row, :, lanes_of(tile)]
                packed = jnp.where(
                    masks.span == 2 * slot, lane_roll(e, 8 * (2 * slot - at)), packed
                )
                packed = jnp.where(
                    masks.span == 2 * slot + 1, lane_roll(n, 8 * (2 * slot + 1 - at)), packed
                )
            span_ref[pack_id, :, lanes_of(tile)] = packed


def take_halos(masks, ends, eq, neq, side_eq, side_neq, east, west, north, south, de, dw):
    for column, speed in enumerate(X_SPEEDS):
        rightward = column < 5
        closed = ends[0 if rightward else 1] == 1
        source, diag, pairs = (east, de, DIAG_EAST) if rightward else (west, dw, DIAG_WEST)
        parts = [(source[column % 5, row], row + 1) for row in range(SPAN_PATCHES)]
        for entry, (diag_speed, row) in enumerate(pairs):
            if diag_speed == speed:
                parts.append((diag[entry], 0 if row else SPAN_PATCHES + 1))
        for packed, row in parts:
            other = lane_roll(packed, 64)
            e, n = (other, packed) if rightward else (packed, other)
            side_eq[column, row] = jnp.where(closed, inflow_value(speed), e)
            side_neq[column, row] = jnp.where(closed, 0.0, n)
    for index, speed in enumerate(Y_SPEEDS):
        from_south = index < 5
        source = north if from_south else south
        row = 0 if from_south else SPAN_PATCHES + 1
        at = 7 if from_south else 0
        slot = index % 4
        for tile in range(TILES):
            packed = source[index // 4, :, lanes_of(tile)]
            eq[speed, row, :, lanes_of(tile)] = lane_roll(packed, 8 * (at - 2 * slot))
            neq[speed, row, :, lanes_of(tile)] = lane_roll(packed, 8 * (at - 2 * slot - 1))


def rates(fine):
    return jnp.where(fine, 1.0 / TAU_FINE, 1.0 / TAU_COARSE)


def open_kernel(level_ref, field_ref, moved_ref, east, west, span, de, dw, eq, neq):
    masks = Masks()

    def row_step(row, carry):
        fine = level_ref[row] == 1
        rate = rates(fine)
        send = jnp.where(fine, 1.0 / RESCALE, 1.0)
        for tile in range(TILES):
            field = []
            for q in range(SPEEDS):
                field.append(field_ref[pl.ds(row * 8, 8), q, lanes_of(tile)])
                moved_ref[q, row, :, lanes_of(tile)] = field[q]
            balance = equilibria(field)
            for q in range(1, SPEEDS):
                relaxed = field[q] + rate * (balance[q] - field[q])
                eq[q, row, :, lanes_of(tile)] = balance[q]
                neq[q, row, :, lanes_of(tile)] = send * (relaxed - balance[q])
        return carry

    lax.fori_loop(0, SPAN_PATCHES, row_step, 0)
    emit_halos(masks, eq, neq, 0, east, west, span, de, dw)


def step_kernel(final, *refs):
    ends, level_ref, field_ref, east, west, north, south, de, dw = refs[:9]
    if final:
        targets, moved_ref = refs[9], refs[10]
        eq, neq, relaxed_ref, side_eq, side_neq, ghost, fresh, again, rows_ref, sems = refs[11:]
    else:
        moved_ref, east_out, west_out, span_out, de_out, dw_out = refs[9:15]
        eq, neq, relaxed_ref, side_eq, side_neq, ghost, fresh, again, eq_next, neq_next = refs[15:]
    masks = Masks()
    take_halos(masks, ends, eq, neq, side_eq, side_neq, east, west, north, south, de, dw)

    def collide_row(row, carry):
        fine = level_ref[row] == 1
        rate = rates(fine)
        send = jnp.where(fine, 1.0 / RESCALE, 1.0)
        for tile in range(TILES):
            field = [field_ref[q, row, :, lanes_of(tile)] for q in range(SPEEDS)]
            balance = equilibria(field)
            for q in range(SPEEDS):
                relaxed = field[q] + rate * (balance[q] - field[q])
                relaxed_ref[q, row, :, lanes_of(tile)] = relaxed
                if q:
                    eq[q, row + 1, :, lanes_of(tile)] = balance[q]
                    neq[q, row + 1, :, lanes_of(tile)] = send * (relaxed - balance[q])
        return carry

    lax.fori_loop(0, SPAN_PATCHES, collide_row, 0)

    def move_row(row, carry):
        fine = level_ref[row] == 1
        scale = jnp.where(fine, RESCALE, 1.0)
        for q in range(SPEEDS):
            _, step_y, step_z = VELOCITIES[q]
            tiles = []
            for tile in range(TILES):
                value = relaxed_ref[q, row, :, lanes_of(tile)]
                across_x, across_y, across_z = masks.leaving(q, tile)

                def source(inner, side, at):
                    picked = inner[q, at, :, lanes_of(tile)]
                    if across_x is not None:
                        picked = jnp.where(across_x, side[X_SPEEDS.index(q), at], picked)
                    return picked

                crossing = masks.leaving_any(q, tile)
                if crossing is not None:
                    pair = []
                    for inner, side in ((eq, side_eq), (neq, side_neq)):
                        picked = source(inner, side, row + 1)
                        if across_y is not None:
                            picked = jnp.where(across_y, source(inner, side, row + 1 - step_y), picked)
                        if across_z is not None:
                            turned = pltpu.roll(picked, step_z % DEPTH_PATCHES, 0)
                            picked = jnp.where(across_z, turned, picked)
                        pair.append(picked)
                    value = jnp.where(crossing, pair[0] + scale * pair[1], value)
                    ghost[q, :, lanes_of(tile)] = value
                tiles.append(value)
            for tile, value in enumerate(masks.shifted(tiles, q)):
                fresh[q, :, lanes_of(tile)] = value
        for tile in range(TILES):
            field = [fresh[q, :, lanes_of(tile)] for q in range(SPEEDS)]
            balance = equilibria(field)
            for q in range(SPEEDS):
                again[q, :, lanes_of(tile)] = field[q] + (1.0 / TAU_FINE) * (balance[q] - field[q])
        for q in range(SPEEDS):
            tiles = []
            for tile in range(TILES):
                value = again[q, :, lanes_of(tile)]
                crossing = masks.leaving_any(q, tile)
                if crossing is not None:
                    value = jnp.where(crossing, ghost[q, :, lanes_of(tile)], value)
                tiles.append(value)
            for tile, value in enumerate(masks.shifted(tiles, q)):
                value = jnp.where(fine, value, fresh[q, :, lanes_of(tile)])
                if final:
                    start = row * (8 * ROWS) + (q * TILES + tile)
                    rows_ref[pl.ds(start, 8, stride=ROWS), :] = value
                else:
                    moved_ref[q, row, :, lanes_of(tile)] = value
        if final:
            for depth in range(8):
                patch_copy(row * 8 + depth).start()
        else:
            rate = rates(fine)
            send = jnp.where(fine, 1.0 / RESCALE, 1.0)
            for tile in range(TILES):
                field = [moved_ref[q, row, :, lanes_of(tile)] for q in range(SPEEDS)]
                balance = equilibria(field)
                for q in range(1, SPEEDS):
                    relaxed = field[q] + rate * (balance[q] - field[q])
                    eq_next[q, row, :, lanes_of(tile)] = balance[q]
                    neq_next[q, row, :, lanes_of(tile)] = send * (relaxed - balance[q])
        return carry

    def patch_copy(patch):
        return pltpu.make_async_copy(
            rows_ref.at[pl.ds(pl.multiple_of(patch * ROWS, 8), ROWS), :],
            moved_ref.at[targets[patch]],
            sems.at[patch],
        )

    lax.fori_loop(0, SPAN_PATCHES, move_row, 0)
    if final:

        def drain(patch, carry):
            patch_copy(patch).wait()
            return carry

        lax.fori_loop(0, SPAN_PATCHES * DEPTH_PATCHES, drain, 0)
    else:
        emit_halos(masks, eq_next, neq_next, 0, east_out, west_out, span_out, de_out, dw_out)


def unpack_kernel(patches, slots, received, out_ref, rows_ref, sems):
    def patch_copy(patch):
        return pltpu.make_async_copy(
            received.at[slots[patch]],
            rows_ref.at[pl.ds(pl.multiple_of(patch * ROWS, 8), ROWS), :],
            sems.at[patch],
        )

    def launch(patch, carry):
        patch_copy(patch).start()
        return carry

    def place(patch, carry):
        patch_copy(patch).wait()
        for first in range(0, SPEEDS, 8):
            count = min(8, SPEEDS - first)
            for tile in range(TILES):
                start = patch * ROWS + (first * TILES + tile)
                out_ref[patch, first : first + count, lanes_of(tile)] = rows_ref[
                    pl.ds(start, count, stride=TILES), :
                ]
        return carry

    lax.fori_loop(0, patches, launch, 0)
    lax.fori_loop(0, patches, place, 0)


def shape(*dims):
    return jax.ShapeDtypeStruct(dims, jnp.float32)


VMEM = pl.BlockSpec(memory_space=pltpu.VMEM)
SMEM = pl.BlockSpec(memory_space=pltpu.SMEM)
ANY = pl.BlockSpec(memory_space=pl.ANY)
PARAMS = pltpu.CompilerParams(vmem_limit_bytes=48 * 1024 * 1024)
FIELD = (SPEEDS, SPAN_PATCHES, DEPTH_PATCHES, CELLS)
FRAMED = (SPEEDS, SPAN_PATCHES + 2, DEPTH_PATCHES, CELLS)
SIDE = (len(X_SPEEDS), SPAN_PATCHES + 2, DEPTH_PATCHES, LANES)
ROW = (SPEEDS, DEPTH_PATCHES, CELLS)
HALOS = (
    shape(5, SPAN_PATCHES, DEPTH_PATCHES, LANES),
    shape(5, SPAN_PATCHES, DEPTH_PATCHES, LANES),
    shape(Y_PACKS, DEPTH_PATCHES, CELLS),
    shape(2, DEPTH_PATCHES, LANES),
    shape(2, DEPTH_PATCHES, LANES),
)


def scratch(dims):
    return pltpu.VMEM(dims, jnp.float32)


def exchange(east, west, span, diag_east, diag_west):
    blocks = lax.axis_size("blocks")
    cross = lax.axis_size("cross")

    def pairs(step_x, step_y):
        return [
            (b * cross + c, (b + step_x) * cross + (c + step_y) % cross)
            for b in range(blocks)
            for c in range(cross)
            if 0 <= b + step_x < blocks
        ]

    def send(value, step_x, step_y):
        return lax.ppermute(value, ("blocks", "cross"), pairs(step_x, step_y))

    def both(value, step_x):
        up = send(value, step_x, 1)
        return up, (up if cross == 2 else send(value, step_x, -1))

    north, south = both(span, 0)
    if cross == 2:
        de = send(diag_east, 1, 1)
        dw = send(diag_west, -1, 1)
    else:
        up, down = both(diag_east, 1)
        de = jnp.stack([up[0], down[1]])
        up, down = both(diag_west, -1)
        dw = jnp.stack([up[0], down[1]])
    return send(east, 1, 0), send(west, -1, 0), north, south, de, dw


def body(f_home, levels, plan):
    devices = lax.axis_size(("blocks", "cross"))
    here = lax.axis_index(("blocks", "cross"))
    patches = f_home.shape[0]
    capacity = (patches + devices - 1) // devices + 1
    block = lax.axis_index("blocks")
    ends = jnp.stack([block == 0, block == lax.axis_size("blocks") - 1]).astype(jnp.int32)
    level_rows = jnp.broadcast_to(
        levels.reshape(SPAN_PATCHES, DEPTH_PATCHES, 1), (SPAN_PATCHES, DEPTH_PATCHES, LANES)
    )

    outs = pl.pallas_call(
        open_kernel,
        out_shape=(shape(*FIELD),) + HALOS,
        in_specs=[VMEM, VMEM],
        out_specs=[VMEM] * 6,
        scratch_shapes=[scratch(FIELD), scratch(FIELD)],
        compiler_params=PARAMS,
        name="open",
    )(level_rows, f_home)
    field, halos = outs[0], exchange(*outs[1:])

    order = jnp.arange(patches, dtype=jnp.int32)
    owner = plan // patches
    earlier = (owner[:, None] == owner[None, :]) & (order[None, :] < order[:, None])
    targets = owner * capacity + jnp.sum(earlier.astype(jnp.int32), axis=1)

    whole_plan = lax.all_gather(plan, ("blocks", "cross"), tiled=True).reshape(devices, patches)
    mine = whole_plan // patches == here
    before = (order[:, None] < order[None, :]).astype(jnp.int32)
    rank = jnp.sum(mine[:, :, None].astype(jnp.int32) * before[None], axis=1)
    slot = jnp.arange(devices, dtype=jnp.int32)[:, None] * capacity + rank
    wanted = whole_plan[None] == (here * patches + order)[:, None, None]
    slots = jnp.sum(jnp.where(wanted, slot[None], 0), axis=(1, 2))

    common = [scratch(FRAMED), scratch(FRAMED), scratch(FIELD), scratch(SIDE), scratch(SIDE)]
    common += [scratch(ROW), scratch(ROW), scratch(ROW)]
    for _ in range(STEPS - 1):
        outs = pl.pallas_call(
            functools.partial(step_kernel, False),
            out_shape=(shape(*FIELD),) + HALOS,
            in_specs=[SMEM] + [VMEM] * 8,
            out_specs=[VMEM] * 6,
            scratch_shapes=common + [scratch(FIELD), scratch(FIELD)],
            compiler_params=PARAMS,
            name="step",
        )(ends, level_rows, field, *halos)
        field, halos = outs[0], exchange(*outs[1:])
    packed = pl.pallas_call(
        functools.partial(step_kernel, True),
        out_shape=shape(devices * capacity, ROWS, LANES),
        in_specs=[SMEM] + [VMEM] * 8 + [SMEM],
        out_specs=ANY,
        scratch_shapes=common
        + [scratch((patches * ROWS, LANES)), pltpu.SemaphoreType.DMA((patches,))],
        compiler_params=PARAMS,
        name="last",
    )(ends, level_rows, field, *halos, targets)
    received = lax.all_to_all(
        packed.reshape(devices, capacity * ROWS, LANES),
        ("blocks", "cross"),
        split_axis=0,
        concat_axis=0,
        tiled=True,
    ).reshape(devices * capacity, ROWS, LANES)
    return pl.pallas_call(
        functools.partial(unpack_kernel, patches),
        out_shape=shape(*f_home.shape),
        in_specs=[SMEM, ANY],
        out_specs=VMEM,
        scratch_shapes=[scratch((patches * ROWS, LANES)), pltpu.SemaphoreType.DMA((patches,))],
        compiler_params=PARAMS,
        name="unpack",
    )(slots, received)


def solution(mesh):
    in_specs = (P(("blocks", "cross"), None, None), P(("blocks", "cross")), P(("blocks", "cross")))
    out_specs = P(("blocks", "cross"), None, None)
    return jax.shard_map(body, mesh=mesh, in_specs=in_specs, out_specs=out_specs, check_vma=False)
```

time: 1200 us -> 155 us (0.13); the launches traced: 1180 us -> 155 us
  local copies, waits for them, and re-layouts: 919 us -> 4.94 us
  other arithmetic: 137 us -> 1.33 us
  waiting for transfers between devices: 94.6 us -> 11.6 us
  blocking collectives: 0 us -> 80.4 us
  Pallas kernels: 0 us -> 25 us
    gather x70 -> x0, local copies, waits for them, and re-layouts: 190 us -> none  [the longest x23 55.4 us: face_payload(): balance[:, list(FACE_SPEEDS[face_id])]]
    slice x61 -> x0, local copies, waits for them, and re-layouts: 170 us -> none  [the longest x28 90 us: neighbour(): return eq_ext[window] + factor * neq_ext[window]]
    unnamed x379 -> x5, local copies, waits for them, and re-layouts: 150 us -> 2.3 us
    scatter x125 -> x0, local copies, waits for them, and re-layouts: 142 us -> none  [the longest x20 35.5 us: propagate(): padded.at[:, speed, 1:extent + 1, 1:extent + 1, 0]]
    unnamed x0 -> x1, blocking collectives: none -> 80.4 us
    reshape x7 -> x0, local copies, waits for them, and re-layouts: 79.4 us -> none  [the longest x2 55.4 us: home_ghosts(): extended = extended.reshape(extended.shape[:3] + (2, 6, 5, EDGE, EDGE))]
    squeeze x25 -> x0, local copies, waits for them, and re-layouts: 70.5 us -> none  [the longest x24 48.1 us: neighbour(): return eq_ext[window] + factor * neq_ext[window]]
    another operation x50 -> x0, local copies, waits for them, and re-layouts: 62.7 us -> none  [the longest x43 62.5 us: propagate(): return jnp.stack(shifted, axis=1)]
  transfers between devices with their start and end apart: 10 -> 11, of which waited for: 5 -> 4; matrix products, arithmetic and copies ran while one was open for 39% -> 1% of each run, Pallas kernels for 0% -> 0%
where the time goes in v1:
time: 155 us
  blocking collectives  80.4 us (52%)
  starting transfers between devices  31.3 us (20%)
  Pallas kernels  25 us (16%)
  waiting for transfers between devices  11.6 us (7%)
  local copies, waits for them, and re-layouts  4.94 us (3%)
    unnamed x1, blocking collectives  80.4 us
    ppermute x10, starting transfers between devices, send(): return lax.ppermute(value, ('blocks', 'cross'), pairs(step_x, step_y))  23.3 us
    ppermute x10, waiting for transfers between devices, send(): return lax.ppermute(value, ('blocks', 'cross'), pairs(step_x, step_y))  11.6 us
    pallas_call x1, Pallas kernels, body(): pl.pallas_call(functools.partial(step_kernel, True), out_shape=shape(devi...  9.14 us
    pallas_call x1, Pallas kernels, body(): pl.pallas_call(functools.partial(step_kernel, False), out_shape=(shape(*F...  8.28 us
    all_to_all x1, starting transfers between devices, body(): lax.all_to_all(packed.reshape(devices, capacity * ROWS, LANES), ('blocks'...  8.04 us
    pallas_call x1, Pallas kernels, body(): pl.pallas_call(open_kernel, out_shape=(shape(*FIELD),) + HALOS, in_specs=...  4.55 us
  transfers between devices with their start and end apart: 11, of which 4 were waited for; matrix products, arithmetic and copies ran while one was open for 1% of the time, Pallas kernels for 0%

profile of v1, /device:TPU:0, one launch (start us, length us, event | category | flops | bytes accessed | tf_op | source)
XLA Modules:
  0.0 154.9 jit_solution(10418433904624584366)
XLA Ops:
  0.0 0.7 broadcast_in_dim.14
  0.7 2.0 %copy.6.field_ref = f32[32,19,512]{2,1,0:T(8,128)S(1)} copy(f32[32,19,512]{2,0,1:T(8,128)} %param.3) | data formatting | bytes 2490368 | tf_op args[0]
  2.8 0.1 broadcast_in_dim.15.level_ref.refs_1_
  2.9 4.5 %open.1 = (f32[19,4,8,512]{3,2,1,0:T(8,128)S(1)}, f32[5,4,8,128]{3,2,1,0:T(8,128)S(1)}, f32[5,4,8,128]{3,2,1,0:T(8,128)S(1)}, f32[3,8,512]{2,1,0:T(8,128)S(1)}, ...) custom-call(s32[4,8,128]{2,1,0:T(8,128)S(1)} %broadcast_in_dim.15.level_ref.refs_1_, f32[32,19,512]{2,1,0:T(8,128)S(1)} %copy.6.field_ref), custom_call_target="tpu_custom_call" | custom-call | tf_op jit(solution)/shard_map/open/pallas_call | solution.py:457
  7.4 4.3 %collective-permute-start.3 = (f32[2,8,128]{2,1,0:T(8,128)S(1)}, f32[2,8,128]{2,1,0:T(8,128)S(1)}, u32[]{:S(2)}, u32[]{:S(2)}) collective-permute-start(f32[2,8,128]{2,1,0:T(8,128)S(1)} %get-tuple-element.21), channel_id=1, source_target_pairs={{0,3},{1,2},{2,5},{3,4},{4,7},{5,6},{6,9},{7,8},{8,11},{9,10},{10,... | collective-permute-start | bytes 24584 | tf_op jit(solution)/shard_map/ppermute | solution.py:428
  11.7 1.3 collective-permute-start.4
  13.0 0.7 collective-permute-start.2
  13.8 4.2 %collective-permute-start = (f32[5,4,8,128]{3,2,1,0:T(8,128)S(1)}, f32[5,4,8,128]{3,2,1,0:T(8,128)S(1)}, u32[]{:S(2)}, u32[]{:S(2)}) collective-permute-start(f32[5,4,8,128]{3,2,1,0:T(8,128)S(1)} %get-tuple-element.18), channel_id=1, source_target_pairs={{0,2},{1,3},{2,4},{3,5},{4,6},{5,7},{6,8},{7,9},{8,10},{9,11},{10,... | collective-permute-start | bytes 245768 | tf_op jit(solution)/shard_map/ppermute | solution.py:428
  17.9 1.3 collective-permute-start.1
  19.3 0.2 convert_reduce_fusion
  19.5 0.1 add_convert_fusion.refs_0_
  19.5 0.0 collective-permute-done.2.refs_5_.refs_6_
  19.6 0.7 collective-permute-done.refs_3_
  20.3 4.8 %collective-permute-done.1.refs_4_ = f32[5,4,8,128]{3,2,1,0:T(8,128)S(1)} collective-permute-done((f32[5,4,8,128]{3,2,1,0:T(8,128)S(1)}, f32[5,4,8,128]{3,2,1,0:T(8,128)S(1)}, u32[]{:S(2)}, u32[]{:S(2)}) %collective-permute-start.1) | collective-permute-done | bytes 81952 | tf_op jit(solution)/shard_map/ppermute | solution.py:428
  25.1 8.3 %step.1 = (f32[19,4,8,512]{3,2,1,0:T(8,128)S(1)}, f32[5,4,8,128]{3,2,1,0:T(8,128)S(1)}, f32[5,4,8,128]{3,2,1,0:T(8,128)S(1)}, f32[3,8,512]{2,1,0:T(8,128)S(1)}, ...) custom-call(s32[2]{0:T(128)S(1)} %add_convert_fusion.refs_0_, s32[4,8,128]{2,1,0:T(8,128)S(1)} %broadcast_in_dim.15.level_ref.refs_1_, ...), custom_call_target="tpu_custom_call" | custom-call | tf_op jit(solution)/shard_map/step/pallas_call | solution.py:484
  33.3 3.5 %collective-permute-start.8 = (f32[2,8,128]{2,1,0:T(8,128)S(1)}, f32[2,8,128]{2,1,0:T(8,128)S(1)}, u32[]{:S(2)}, u32[]{:S(2)}) collective-permute-start(f32[2,8,128]{2,1,0:T(8,128)S(1)} %get-tuple-element.27), channel_id=1, source_target_pairs={{0,3},{1,2},{2,5},{3,4},{4,7},{5,6},{6,9},{7,8},{8,11},{9,10},{10,... | collective-permute-start | bytes 24584 | tf_op jit(solution)/shard_map/ppermute | solution.py:428
  36.8 1.3 collective-permute-start.9
  38.1 1.2 collective-permute-start.7
  39.4 4.2 %collective-permute-start.5 = (f32[5,4,8,128]{3,2,1,0:T(8,128)S(1)}, f32[5,4,8,128]{3,2,1,0:T(8,128)S(1)}, u32[]{:S(2)}, u32[]{:S(2)}) collective-permute-start(f32[5,4,8,128]{3,2,1,0:T(8,128)S(1)} %get-tuple-element.24), channel_id=1, source_target_pairs={{0,2},{1,3},{2,4},{3,5},{4,6},{5,7},{6,8},{7,9},{8,10},{9,11},{10,... | collective-permute-start | bytes 245768 | tf_op jit(solution)/shard_map/ppermute | solution.py:428
  43.5 1.3 collective-permute-start.6
  44.9 1.0 collective-permute-done.5.refs_3_
  45.9 5.1 %collective-permute-done.6.refs_4_ = f32[5,4,8,128]{3,2,1,0:T(8,128)S(1)} collective-permute-done((f32[5,4,8,128]{3,2,1,0:T(8,128)S(1)}, f32[5,4,8,128]{3,2,1,0:T(8,128)S(1)}, u32[]{:S(2)}, u32[]{:S(2)}) %collective-permute-start.6) | collective-permute-done | bytes 81952 | tf_op jit(solution)/shard_map/ppermute | solution.py:428
  51.0 9.1 %last.1 = f32[64,80,128]{2,1,0:T(8,128)} custom-call(s32[2]{0:T(128)S(1)} %add_convert_fusion.refs_0_, s32[4,8,128]{2,1,0:T(8,128)S(1)} %broadcast_in_dim.15.level_ref.refs_1_, f32[19,4,8,512]{3,2,1,0:T(8,128)S(1)} %get-tuple-element.23.refs_2_, f32[5,4,8,128]{3,2,1,0:T(8,128)S(1)} %collective-permute-done.5.refs_3_, ...), custom_call_target="tpu_custom_call" | custom-call | tf_op jit(solution)/shard_map/last/pallas_call | solution.py:494
  60.2 8.0 %all-to-all-start = ((f32[32,160,128]{2,1,0:T(8,128)}), f32[32,160,128]{2,1,0:T(8,128)S(1)}, u32[]{:S(2)}, u32[]{:S(2)}) async-start(f32[32,160,128]{2,1,0:T(8,128)} %bitcast.2), calls=%async_computation | async-start | bytes 5242880 | tf_op jit(solution)/shard_map/all_to_all | solution.py:504
  68.2 0.2 dynamic-update-slice
  68.5 80.4 %all-reduce = s32[1024]{0:T(1024)S(1)} all-reduce(s32[1024]{0:T(1024)S(1)} %dynamic-update-slice), channel_id=1, replica_groups=mesh['blocks'=16,'cross'=2] {'blocks','cross'}, use_global_device_ids=true, to_apply=%add | all-reduce | flops 1024 | bytes 8192
  148.9 0.1 eq.44
  149.0 0.2 multiply_reduce_fusion
  149.2 0.1 broadcast_add_fusion
  149.3 0.7 select_reduce_fusion.slots
  150.0 3.1 %unpack.1 = f32[32,19,512]{2,1,0:T(8,128)S(1)} custom-call(s32[32]{0:T(128)S(1)} %select_reduce_fusion.slots, f32[64,80,128]{2,1,0:T(8,128)S(1)} %bitcast.4), custom_call_target="tpu_custom_call" | custom-call | tf_op jit(solution)/shard_map/unpack/pallas_call | solution.py:511
  153.1 1.8 %copy.7 = f32[32,19,512]{2,0,1:T(8,128)} copy(f32[32,19,512]{2,1,0:T(8,128)S(1)} %unpack.1) | data formatting | bytes 2490368 | tf_op jit(solution)/shard_map/unpack/pallas_call | solution.py:511
  (15 shorter events, 0.1 us)
Async XLA Ops:
  0.7 18.5 %copy-start = (s32[32]{0:T(128)S(1)}, s32[32]{0:T(128)}, u32[]{:S(2)}) copy-start(s32[32]{0:T(128)} %param.5) | copy-start | bytes 388
  7.4 12.1 %collective-permute-start.3 = (f32[2,8,128]{2,1,0:T(8,128)S(1)}, f32[2,8,128]{2,1,0:T(8,128)S(1)}, u32[]{:S(2)}, u32[]{:S(2)}) collective-permute-start(f32[2,8,128]{2,1,0:T(8,128)S(1)} %get-tuple-element.21), channel_id=1, source_target_pairs={{0,3},{1,2},{2,5},{3,4},{4,7},{5,6},{6,9},{7,8},{8,11},{9,10},{10,... | collective-permute-start | bytes 24584 | tf_op jit(solution)/shard_map/ppermute | solution.py:428
  11.7 7.8 %collective-permute-start.4 = (f32[2,8,128]{2,1,0:T(8,128)S(1)}, f32[2,8,128]{2,1,0:T(8,128)S(1)}, u32[]{:S(2)}, u32[]{:S(2)}) collective-permute-start(f32[2,8,128]{2,1,0:T(8,128)S(1)} %get-tuple-element.22), channel_id=1, source_target_pairs={{2,1},{3,0},{4,3},{5,2},{6,5},{7,4},{8,7},{9,6},{10,9},{11,8},{12,... | collective-permute-start | bytes 24584 | tf_op jit(solution)/shard_map/ppermute | solution.py:428
  13.0 6.5 %collective-permute-start.2 = (f32[3,8,512]{2,1,0:T(8,128)S(1)}, f32[3,8,512]{2,1,0:T(8,128)S(1)}, u32[]{:S(2)}, u32[]{:S(2)}) collective-permute-start(f32[3,8,512]{2,1,0:T(8,128)S(1)} %get-tuple-element.20), channel_id=1, source_target_pairs={{0,1},{1,0},{2,3},{3,2},{4,5},{5,4},{6,7},{7,6},{8,9},{9,8},{10,11... | collective-permute-start | bytes 147464 | tf_op jit(solution)/shard_map/ppermute | solution.py:428
  13.8 6.5 %collective-permute-start = (f32[5,4,8,128]{3,2,1,0:T(8,128)S(1)}, f32[5,4,8,128]{3,2,1,0:T(8,128)S(1)}, u32[]{:S(2)}, u32[]{:S(2)}) collective-permute-start(f32[5,4,8,128]{3,2,1,0:T(8,128)S(1)} %get-tuple-element.18), channel_id=1, source_target_pairs={{0,2},{1,3},{2,4},{3,5},{4,6},{5,7},{6,8},{7,9},{8,10},{9,11},{10,... | collective-permute-start | bytes 245768 | tf_op jit(solution)/shard_map/ppermute | solution.py:428
  17.9 7.1 %collective-permute-start.1 = (f32[5,4,8,128]{3,2,1,0:T(8,128)S(1)}, f32[5,4,8,128]{3,2,1,0:T(8,128)S(1)}, u32[]{:S(2)}, u32[]{:S(2)}) collective-permute-start(f32[5,4,8,128]{3,2,1,0:T(8,128)S(1)} %get-tuple-element.19), channel_id=1, source_target_pairs={{2,0},{3,1},{4,2},{5,3},{6,4},{7,5},{8,6},{9,7},{10,8},{11,9},{12,... | collective-permute-start | bytes 245768 | tf_op jit(solution)/shard_map/ppermute | solution.py:428
  33.3 11.5 %collective-permute-start.8 = (f32[2,8,128]{2,1,0:T(8,128)S(1)}, f32[2,8,128]{2,1,0:T(8,128)S(1)}, u32[]{:S(2)}, u32[]{:S(2)}) collective-permute-start(f32[2,8,128]{2,1,0:T(8,128)S(1)} %get-tuple-element.27), channel_id=1, source_target_pairs={{0,3},{1,2},{2,5},{3,4},{4,7},{5,6},{6,9},{7,8},{8,11},{9,10},{10,... | collective-permute-start | bytes 24584 | tf_op jit(solution)/shard_map/ppermute | solution.py:428
  36.8 8.0 %collective-permute-start.9 = (f32[2,8,128]{2,1,0:T(8,128)S(1)}, f32[2,8,128]{2,1,0:T(8,128)S(1)}, u32[]{:S(2)}, u32[]{:S(2)}) collective-permute-start(f32[2,8,128]{2,1,0:T(8,128)S(1)} %get-tuple-element.28), channel_id=1, source_target_pairs={{2,1},{3,0},{4,3},{5,2},{6,5},{7,4},{8,7},{9,6},{10,9},{11,8},{12,... | collective-permute-start | bytes 24584 | tf_op jit(solution)/shard_map/ppermute | solution.py:428
  38.1 6.7 %collective-permute-start.7 = (f32[3,8,512]{2,1,0:T(8,128)S(1)}, f32[3,8,512]{2,1,0:T(8,128)S(1)}, u32[]{:S(2)}, u32[]{:S(2)}) collective-permute-start(f32[3,8,512]{2,1,0:T(8,128)S(1)} %get-tuple-element.26), channel_id=1, source_target_pairs={{0,1},{1,0},{2,3},{3,2},{4,5},{5,4},{6,7},{7,6},{8,9},{9,8},{10,11... | collective-permute-start | bytes 147464 | tf_op jit(solution)/shard_map/ppermute | solution.py:428
  39.4 6.5 %collective-permute-start.5 = (f32[5,4,8,128]{3,2,1,0:T(8,128)S(1)}, f32[5,4,8,128]{3,2,1,0:T(8,128)S(1)}, u32[]{:S(2)}, u32[]{:S(2)}) collective-permute-start(f32[5,4,8,128]{3,2,1,0:T(8,128)S(1)} %get-tuple-element.24), channel_id=1, source_target_pairs={{0,2},{1,3},{2,4},{3,5},{4,6},{5,7},{6,8},{7,9},{8,10},{9,11},{10,... | collective-permute-start | bytes 245768 | tf_op jit(solution)/shard_map/ppermute | solution.py:428
  43.5 7.5 %collective-permute-start.6 = (f32[5,4,8,128]{3,2,1,0:T(8,128)S(1)}, f32[5,4,8,128]{3,2,1,0:T(8,128)S(1)}, u32[]{:S(2)}, u32[]{:S(2)}) collective-permute-start(f32[5,4,8,128]{3,2,1,0:T(8,128)S(1)} %get-tuple-element.25), channel_id=1, source_target_pairs={{2,0},{3,1},{4,2},{5,3},{6,4},{7,5},{8,6},{9,7},{10,8},{11,9},{12,... | collective-permute-start | bytes 245768 | tf_op jit(solution)/shard_map/ppermute | solution.py:428
  60.2 89.9 %all-to-all-start = ((f32[32,160,128]{2,1,0:T(8,128)}), f32[32,160,128]{2,1,0:T(8,128)S(1)}, u32[]{:S(2)}, u32[]{:S(2)}) async-start(f32[32,160,128]{2,1,0:T(8,128)} %bitcast.2), calls=%async_computation | async-start | bytes 5242880 | tf_op jit(solution)/shard_map/all_to_all | solution.py:504

commit v2 on v1

--- a/solution.py
+++ b/solution.py
@@ -151,27 +151,27 @@
     return pl.ds(tile * LANES, LANES)
 
 
-def emit_halos(masks, eq, neq, base, east_ref, west_ref, span_ref, diag_east_ref, diag_west_ref):
+def emit_halos(masks, eq, neq, east_ref, west_ref, span_ref):
     last = TILES - 1
 
     def east_pack(speed, row):
-        e = eq[speed, base + row, :, lanes_of(last)]
-        n = neq[speed, base + row, :, lanes_of(last)]
+        e = eq[speed, row, :, lanes_of(last)]
+        n = neq[speed, row, :, lanes_of(last)]
         return jnp.where(masks.low, lane_roll(e, 64), n)
 
     def west_pack(speed, row):
-        e = eq[speed, base + row, :, lanes_of(0)]
-        n = neq[speed, base + row, :, lanes_of(0)]
+        e = eq[speed, row, :, lanes_of(0)]
+        n = neq[speed, row, :, lanes_of(0)]
         return jnp.where(masks.low, e, lane_roll(n, 64))
 
     for column in range(5):
         for row in range(SPAN_PATCHES):
-            east_ref[column, row] = east_pack(EAST[column], row)
-            west_ref[column, row] = west_pack(WEST[column], row)
+            east_ref[column * SPAN_PATCHES + row] = east_pack(EAST[column], row)
+            west_ref[column * SPAN_PATCHES + row] = west_pack(WEST[column], row)
     for column, (speed, row) in enumerate(DIAG_EAST):
-        diag_east_ref[column] = east_pack(speed, row)
+        span_ref[Y_PACKS * TILES + column] = east_pack(speed, row)
     for column, (speed, row) in enumerate(DIAG_WEST):
-        diag_west_ref[column] = west_pack(speed, row)
+        span_ref[Y_PACKS * TILES + 2 + column] = west_pack(speed, row)
     for pack_id in range(Y_PACKS):
         for tile in range(TILES):
             packed = jnp.zeros((8, LANES), jnp.float32)
@@ -180,7 +180,7 @@
                 if index >= len(Y_SPEEDS):
                     continue
                 north = index < 5
-                row = base + (SPAN_PATCHES - 1 if north else 0)
+                row = SPAN_PATCHES - 1 if north else 0
                 at = 7 if north else 0
                 e = eq[Y_SPEEDS[index], row, :, lanes_of(tile)]
                 n = neq[Y_SPEEDS[index], row, :, lanes_of(tile)]
@@ -190,89 +190,75 @@
                 packed = jnp.where(
                     masks.span == 2 * slot + 1, lane_roll(n, 8 * (2 * slot + 1 - at)), packed
                 )
-            span_ref[pack_id, :, lanes_of(tile)] = packed
-
-
-def take_halos(masks, ends, eq, neq, side_eq, side_neq, east, west, north, south, de, dw):
+            span_ref[pack_id * TILES + tile] = packed
+
+
+def take_halos(ends, span_eq, span_neq, side_eq, side_neq, east, west, north, south):
     for column, speed in enumerate(X_SPEEDS):
         rightward = column < 5
         closed = ends[0 if rightward else 1] == 1
-        source, diag, pairs = (east, de, DIAG_EAST) if rightward else (west, dw, DIAG_WEST)
-        parts = [(source[column % 5, row], row + 1) for row in range(SPAN_PATCHES)]
+        source, pairs = (east, DIAG_EAST) if rightward else (west, DIAG_WEST)
+        first = column % 5 * SPAN_PATCHES
+        parts = [(source[first + row], row + 1) for row in range(SPAN_PATCHES)]
         for entry, (diag_speed, row) in enumerate(pairs):
             if diag_speed == speed:
-                parts.append((diag[entry], 0 if row else SPAN_PATCHES + 1))
+                parts.append((source[5 * SPAN_PATCHES + entry], 0 if row else SPAN_PATCHES + 1))
         for packed, row in parts:
             other = lane_roll(packed, 64)
             e, n = (other, packed) if rightward else (packed, other)
             side_eq[column, row] = jnp.where(closed, inflow_value(speed), e)
             side_neq[column, row] = jnp.where(closed, 0.0, n)
-    for index, speed in enumerate(Y_SPEEDS):
+    for index in range(len(Y_SPEEDS)):
         from_south = index < 5
         source = north if from_south else south
-        row = 0 if from_south else SPAN_PATCHES + 1
         at = 7 if from_south else 0
         slot = index % 4
         for tile in range(TILES):
-            packed = source[index // 4, :, lanes_of(tile)]
-            eq[speed, row, :, lanes_of(tile)] = lane_roll(packed, 8 * (at - 2 * slot))
-            neq[speed, row, :, lanes_of(tile)] = lane_roll(packed, 8 * (at - 2 * slot - 1))
+            packed = source[index // 4 * TILES + tile]
+            span_eq[index, :, lanes_of(tile)] = lane_roll(packed, 8 * (at - 2 * slot))
+            span_neq[index, :, lanes_of(tile)] = lane_roll(packed, 8 * (at - 2 * slot - 1))
 
 
 def rates(fine):
     return jnp.where(fine, 1.0 / TAU_FINE, 1.0 / TAU_COARSE)
 
 
-def open_kernel(level_ref, field_ref, moved_ref, east, west, span, de, dw, eq, neq):
+def relax(masks, field, fine, row, tile, relaxed_ref, eq, neq):
+    balance = equilibria(field)
+    rate = rates(fine)
+    send = jnp.where(fine, 1.0 / RESCALE, 1.0)
+    for q in range(SPEEDS):
+        relaxed = field[q] + rate * (balance[q] - field[q])
+        relaxed_ref[q, row, :, lanes_of(tile)] = relaxed
+        if q:
+            eq[q, row, :, lanes_of(tile)] = balance[q]
+            neq[q, row, :, lanes_of(tile)] = send * (relaxed - balance[q])
+
+
+def open_kernel(level_ref, field_ref, relaxed_ref, eq, neq, east, west, span):
     masks = Masks()
 
     def row_step(row, carry):
         fine = level_ref[row] == 1
-        rate = rates(fine)
-        send = jnp.where(fine, 1.0 / RESCALE, 1.0)
         for tile in range(TILES):
-            field = []
-            for q in range(SPEEDS):
-                field.append(field_ref[pl.ds(row * 8, 8), q, lanes_of(tile)])
-                moved_ref[q, row, :, lanes_of(tile)] = field[q]
-            balance = equilibria(field)
-            for q in range(1, SPEEDS):
-                relaxed = field[q] + rate * (balance[q] - field[q])
-                eq[q, row, :, lanes_of(tile)] = balance[q]
-                neq[q, row, :, lanes_of(tile)] = send * (relaxed - balance[q])
+            field = [field_ref[pl.ds(row * 8, 8), q, lanes_of(tile)] for q in range(SPEEDS)]
+            relax(masks, field, fine, row, tile, relaxed_ref, eq, neq)
         return carry
 
     lax.fori_loop(0, SPAN_PATCHES, row_step, 0)
-    emit_halos(masks, eq, neq, 0, east, west, span, de, dw)
+    emit_halos(masks, eq, neq, east, west, span)
 
 
 def step_kernel(final, *refs):
-    ends, level_ref, field_ref, east, west, north, south, de, dw = refs[:9]
+    ends, level_ref, relaxed_ref, eq, neq, east, west, north, south = refs[:9]
     if final:
-        targets, moved_ref = refs[9], refs[10]
-        eq, neq, relaxed_ref, side_eq, side_neq, ghost, fresh, again, rows_ref, sems = refs[11:]
+        targets, _, moved_ref = refs[9:12]
+        span_eq, span_neq, side_eq, side_neq, ghost, fresh, again, rows_ref, sems = refs[12:]
     else:
-        moved_ref, east_out, west_out, span_out, de_out, dw_out = refs[9:15]
-        eq, neq, relaxed_ref, side_eq, side_neq, ghost, fresh, again, eq_next, neq_next = refs[15:]
+        relaxed_next, eq_next, neq_next, east_out, west_out, span_out = refs[9:15]
+        span_eq, span_neq, side_eq, side_neq, ghost, fresh, again = refs[15:]
     masks = Masks()
-    take_halos(masks, ends, eq, neq, side_eq, side_neq, east, west, north, south, de, dw)
-
-    def collide_row(row, carry):
-        fine = level_ref[row] == 1
-        rate = rates(fine)
-        send = jnp.where(fine, 1.0 / RESCALE, 1.0)
-        for tile in range(TILES):
-            field = [field_ref[q, row, :, lanes_of(tile)] for q in range(SPEEDS)]
-            balance = equilibria(field)
-            for q in range(SPEEDS):
-                relaxed = field[q] + rate * (balance[q] - field[q])
-                relaxed_ref[q, row, :, lanes_of(tile)] = relaxed
-                if q:
-                    eq[q, row + 1, :, lanes_of(tile)] = balance[q]
-                    neq[q, row + 1, :, lanes_of(tile)] = send * (relaxed - balance[q])
-        return carry
-
-    lax.fori_loop(0, SPAN_PATCHES, collide_row, 0)
+    take_halos(ends, span_eq, span_neq, side_eq, side_neq, east, west, north, south)
 
     def move_row(row, carry):
         fine = level_ref[row] == 1
@@ -284,19 +270,26 @@
                 value = relaxed_ref[q, row, :, lanes_of(tile)]
                 across_x, across_y, across_z = masks.leaving(q, tile)
 
-                def source(inner, side, at):
-                    picked = inner[q, at, :, lanes_of(tile)]
+                def source(inner, side, outer, step_y):
+                    at = row - step_y
+                    if step_y:
+                        beyond = outer[Y_SPEEDS.index(q), :, lanes_of(tile)]
+                        inside = inner[q, jnp.clip(at, 0, SPAN_PATCHES - 1), :, lanes_of(tile)]
+                        edge = 0 if step_y == 1 else SPAN_PATCHES - 1
+                        picked = jnp.where(row == edge, beyond, inside)
+                    else:
+                        picked = inner[q, at, :, lanes_of(tile)]
                     if across_x is not None:
-                        picked = jnp.where(across_x, side[X_SPEEDS.index(q), at], picked)
+                        picked = jnp.where(across_x, side[X_SPEEDS.index(q), at + 1], picked)
                     return picked
 
                 crossing = masks.leaving_any(q, tile)
                 if crossing is not None:
                     pair = []
-                    for inner, side in ((eq, side_eq), (neq, side_neq)):
-                        picked = source(inner, side, row + 1)
+                    for group in ((eq, side_eq, span_eq), (neq, side_neq, span_neq)):
+                        picked = source(*group, 0)
                         if across_y is not None:
-                            picked = jnp.where(across_y, source(inner, side, row + 1 - step_y), picked)
+                            picked = jnp.where(across_y, source(*group, step_y), picked)
                         if across_z is not None:
                             turned = pltpu.roll(picked, step_z % DEPTH_PATCHES, 0)
                             picked = jnp.where(across_z, turned, picked)
@@ -325,20 +318,14 @@
                     start = row * (8 * ROWS) + (q * TILES + tile)
                     rows_ref[pl.ds(start, 8, stride=ROWS), :] = value
                 else:
-                    moved_ref[q, row, :, lanes_of(tile)] = value
+                    fresh[q, :, lanes_of(tile)] = value
         if final:
             for depth in range(8):
                 patch_copy(row * 8 + depth).start()
         else:
-            rate = rates(fine)
-            send = jnp.where(fine, 1.0 / RESCALE, 1.0)
             for tile in range(TILES):
-                field = [moved_ref[q, row, :, lanes_of(tile)] for q in range(SPEEDS)]
-                balance = equilibria(field)
-                for q in range(1, SPEEDS):
-                    relaxed = field[q] + rate * (balance[q] - field[q])
-                    eq_next[q, row, :, lanes_of(tile)] = balance[q]
-                    neq_next[q, row, :, lanes_of(tile)] = send * (relaxed - balance[q])
+                field = [fresh[q, :, lanes_of(tile)] for q in range(SPEEDS)]
+                relax(masks, field, fine, row, tile, relaxed_next, eq_next, neq_next)
         return carry
 
     def patch_copy(patch):
@@ -357,7 +344,7 @@
 
         lax.fori_loop(0, SPAN_PATCHES * DEPTH_PATCHES, drain, 0)
     else:
-        emit_halos(masks, eq_next, neq_next, 0, east_out, west_out, span_out, de_out, dw_out)
+        emit_halos(masks, eq_next, neq_next, east_out, west_out, span_out)
 
 
 def unpack_kernel(patches, slots, received, out_ref, rows_ref, sems):
@@ -394,17 +381,18 @@
 VMEM = pl.BlockSpec(memory_space=pltpu.VMEM)
 SMEM = pl.BlockSpec(memory_space=pltpu.SMEM)
 ANY = pl.BlockSpec(memory_space=pl.ANY)
-PARAMS = pltpu.CompilerParams(vmem_limit_bytes=48 * 1024 * 1024)
+PARAMS = pltpu.CompilerParams(vmem_limit_bytes=16 * 1024 * 1024)
 FIELD = (SPEEDS, SPAN_PATCHES, DEPTH_PATCHES, CELLS)
-FRAMED = (SPEEDS, SPAN_PATCHES + 2, DEPTH_PATCHES, CELLS)
 SIDE = (len(X_SPEEDS), SPAN_PATCHES + 2, DEPTH_PATCHES, LANES)
 ROW = (SPEEDS, DEPTH_PATCHES, CELLS)
-HALOS = (
-    shape(5, SPAN_PATCHES, DEPTH_PATCHES, LANES),
-    shape(5, SPAN_PATCHES, DEPTH_PATCHES, LANES),
-    shape(Y_PACKS, DEPTH_PATCHES, CELLS),
-    shape(2, DEPTH_PATCHES, LANES),
-    shape(2, DEPTH_PATCHES, LANES),
+SPAN = (len(X_SPEEDS), DEPTH_PATCHES, CELLS)
+HANDED = (
+    shape(*FIELD),
+    shape(*FIELD),
+    shape(*FIELD),
+    shape(5 * SPAN_PATCHES, DEPTH_PATCHES, LANES),
+    shape(5 * SPAN_PATCHES, DEPTH_PATCHES, LANES),
+    shape(Y_PACKS * TILES + 4, DEPTH_PATCHES, LANES),
 )
 
 
@@ -412,35 +400,28 @@
     return pltpu.VMEM(dims, jnp.float32)
 
 
-def exchange(east, west, span, diag_east, diag_west):
+def exchange(east, west, span):
     blocks = lax.axis_size("blocks")
     cross = lax.axis_size("cross")
 
-    def pairs(step_x, step_y):
-        return [
-            (b * cross + c, (b + step_x) * cross + (c + step_y) % cross)
-            for b in range(blocks)
-            for c in range(cross)
-            if 0 <= b + step_x < blocks
-        ]
-
-    def send(value, step_x, step_y):
-        return lax.ppermute(value, ("blocks", "cross"), pairs(step_x, step_y))
-
-    def both(value, step_x):
-        up = send(value, step_x, 1)
-        return up, (up if cross == 2 else send(value, step_x, -1))
-
-    north, south = both(span, 0)
+    def send_span(step):
+        return lax.ppermute(span, "cross", [(c, (c + step) % cross) for c in range(cross)])
+
+    def send_flow(value, corner, step):
+        whole = jnp.concatenate([value, corner])
+        pairs = [(b, b + step) for b in range(blocks) if 0 <= b + step < blocks]
+        return lax.ppermute(whole, "blocks", pairs)
+
+    north = send_span(1)
+    south = north if cross == 2 else send_span(-1)
+    first = Y_PACKS * TILES
+    corners = [north[first : first + 1], south[first + 1 : first + 2]]
+    corners += [north[first + 2 : first + 3], south[first + 3 : first + 4]]
     if cross == 2:
-        de = send(diag_east, 1, 1)
-        dw = send(diag_west, -1, 1)
+        corner_east, corner_west = north[first : first + 2], north[first + 2 : first + 4]
     else:
-        up, down = both(diag_east, 1)
-        de = jnp.stack([up[0], down[1]])
-        up, down = both(diag_west, -1)
-        dw = jnp.stack([up[0], down[1]])
-    return send(east, 1, 0), send(west, -1, 0), north, south, de, dw
+        corner_east, corner_west = jnp.concatenate(corners[:2]), jnp.concatenate(corners[2:])
+    return send_flow(east, corner_east, 1), send_flow(west, corner_west, -1), north, south
 
 
 def body(f_home, levels, plan):
@@ -454,53 +435,51 @@
         levels.reshape(SPAN_PATCHES, DEPTH_PATCHES, 1), (SPAN_PATCHES, DEPTH_PATCHES, LANES)
     )
 
-    outs = pl.pallas_call(
-        open_kernel,
-        out_shape=(shape(*FIELD),) + HALOS,
-        in_specs=[VMEM, VMEM],
-        out_specs=[VMEM] * 6,
-        scratch_shapes=[scratch(FIELD), scratch(FIELD)],
-        compiler_params=PARAMS,
-        name="open",
-    )(level_rows, f_home)
-    field, halos = outs[0], exchange(*outs[1:])
-
     order = jnp.arange(patches, dtype=jnp.int32)
     owner = plan // patches
     earlier = (owner[:, None] == owner[None, :]) & (order[None, :] < order[:, None])
     targets = owner * capacity + jnp.sum(earlier.astype(jnp.int32), axis=1)
-
-    whole_plan = lax.all_gather(plan, ("blocks", "cross"), tiled=True).reshape(devices, patches)
-    mine = whole_plan // patches == here
-    before = (order[:, None] < order[None, :]).astype(jnp.int32)
-    rank = jnp.sum(mine[:, :, None].astype(jnp.int32) * before[None], axis=1)
-    slot = jnp.arange(devices, dtype=jnp.int32)[:, None] * capacity + rank
-    wanted = whole_plan[None] == (here * patches + order)[:, None, None]
-    slots = jnp.sum(jnp.where(wanted, slot[None], 0), axis=(1, 2))
-
-    common = [scratch(FRAMED), scratch(FRAMED), scratch(FIELD), scratch(SIDE), scratch(SIDE)]
+    table_order = jnp.arange(devices * capacity, dtype=jnp.int32)
+    table = jnp.sum(
+        jnp.where(targets[None, :] == table_order[:, None], plan[None, :] % patches + 1, 0), axis=1
+    )
+    table = lax.all_to_all(
+        table.reshape(devices, capacity), ("blocks", "cross"), 0, 0, tiled=True
+    ).reshape(devices * capacity)
+    slots = jnp.sum(
+        jnp.where(table[None, :] == order[:, None] + 1, table_order[None, :], 0), axis=1
+    )
+
+    outs = pl.pallas_call(
+        open_kernel,
+        out_shape=HANDED,
+        in_specs=[VMEM, VMEM],
+        out_specs=[VMEM] * 6,
+        compiler_params=PARAMS,
+        name="open",
+    )(level_rows, f_home)
+    common = [scratch(SPAN), scratch(SPAN), scratch(SIDE), scratch(SIDE)]
     common += [scratch(ROW), scratch(ROW), scratch(ROW)]
     for _ in range(STEPS - 1):
         outs = pl.pallas_call(
             functools.partial(step_kernel, False),
-            out_shape=(shape(*FIELD),) + HALOS,
+            out_shape=HANDED,
             in_specs=[SMEM] + [VMEM] * 8,
             out_specs=[VMEM] * 6,
-            scratch_shapes=common + [scratch(FIELD), scratch(FIELD)],
+            scratch_shapes=common,
             compiler_params=PARAMS,
             name="step",
-        )(ends, level_rows, field, *halos)
-        field, halos = outs[0], exchange(*outs[1:])
+        )(ends, level_rows, *outs[:3], *exchange(*outs[3:]))
     packed = pl.pallas_call(
         functools.partial(step_kernel, True),
         out_shape=shape(devices * capacity, ROWS, LANES),
-        in_specs=[SMEM] + [VMEM] * 8 + [SMEM],
+        in_specs=[SMEM] + [VMEM] * 8 + [SMEM, SMEM],
         out_specs=ANY,
         scratch_shapes=common
         + [scratch((patches * ROWS, LANES)), pltpu.SemaphoreType.DMA((patches,))],
         compiler_params=PARAMS,
         name="last",
-    )(ends, level_rows, field, *halos, targets)
+    )(ends, level_rows, *outs[:3], *exchange(*outs[3:]), targets, slots)
     received = lax.all_to_all(
         packed.reshape(devices, capacity * ROWS, LANES),
         ("blocks", "cross"),

time: 155 us -> 137 us (0.88)
  blocking collectives: 80.4 us -> 67.2 us
  starting transfers between devices: 31.3 us -> 19.6 us
  local copies, waits for them, and re-layouts: 4.94 us -> 15.3 us
  waiting for transfers between devices: 11.6 us -> 7.87 us
    unnamed x1 -> x0, blocking collectives: 80.4 us -> none
    all_to_all x0 -> x1, blocking collectives: none -> 67.2 us  [body(): lax.all_to_all(packed.reshape(devices, capacity * ROWS, LANES), ('blocks'...]
    ppermute x10 -> x6, starting transfers between devices: 23.3 us -> 12.7 us  [the longest x4 12.2 us: send_flow(): return lax.ppermute(whole, 'blocks', pairs)]
    unnamed x5 -> x19, local copies, waits for them, and re-layouts: 2.3 us -> 11.4 us
    ppermute x10 -> x6, waiting for transfers between devices: 11.6 us -> 7.87 us  [the longest x4 7.86 us: send_flow(): return lax.ppermute(whole, 'blocks', pairs)]
  transfers between devices with their start and end apart: 11 -> 7, of which waited for: 4 -> 4; matrix products, arithmetic and copies ran while one was open for 1% -> 1% of each run, Pallas kernels for 0% -> 6%
where the time goes in v2:
time: 137 us
  blocking collectives  67.2 us (49%)
  Pallas kernels  25.3 us (18%)
  starting transfers between devices  19.6 us (14%)
  local copies, waits for them, and re-layouts  15.3 us (11%)
  waiting for transfers between devices  7.87 us (6%)
    all_to_all x1, blocking collectives, body(): lax.all_to_all(packed.reshape(devices, capacity * ROWS, LANES), ('blocks'...  67.2 us
    ppermute x4, starting transfers between devices, send_flow(): return lax.ppermute(whole, 'blocks', pairs)  12.2 us
    unnamed x19, local copies, waits for them, and re-layouts  11.4 us
    pallas_call x1, Pallas kernels, body(): pl.pallas_call(functools.partial(step_kernel, True), out_shape=shape(devi...  10.1 us
    ppermute x4, waiting for transfers between devices, send_flow(): return lax.ppermute(whole, 'blocks', pairs)  7.86 us
    pallas_call x1, Pallas kernels, body(): pl.pallas_call(functools.partial(step_kernel, False), out_shape=HANDED, i...  7.69 us
    all_to_all x1, starting transfers between devices, body(): lax.all_to_all(table.reshape(devices, capacity), ('blocks', 'cross'), 0,...  6.95 us
    pallas_call x1, Pallas kernels, body(): pl.pallas_call(open_kernel, out_shape=HANDED, in_specs=[VMEM, VMEM], out_...  4.46 us
  transfers between devices with their start and end apart: 7, of which 4 were waited for; matrix products, arithmetic and copies ran while one was open for 1% of the time, Pallas kernels for 6%

profile of v2, /device:TPU:0, one launch (start us, length us, event | category | flops | bytes accessed | tf_op | source)
XLA Modules:
  0.0 136.7 jit_solution(14388482119855875587)
XLA Ops:
  0.0 0.7 broadcast_in_dim.44
  0.7 2.0 %copy.12.field_ref = f32[32,19,512]{2,1,0:T(8,128)S(1)} copy(f32[32,19,512]{2,0,1:T(8,128)} %param.3) | data formatting | bytes 2490368 | tf_op args[0]
  2.9 4.5 %open.1 = (f32[19,4,8,512]{3,2,1,0:T(8,128)S(1)}, f32[19,4,8,512]{3,2,1,0:T(8,128)S(1)}, f32[19,4,8,512]{3,2,1,0:T(8,128)S(1)}, f32[20,8,128]{2,1,0:T(8,128)S(1)...) custom-call(s32[4,8,128]{2,1,0:T(8,128)S(1)} %broadcast_in_dim.45.level_ref.refs_1_, ...), custom_call_target="tpu_custom_call" | custom-call | tf_op jit(solution)/shard_map/open/pallas_call | solution.py:453
  7.3 1.0 copy-done
  8.4 0.5 collective-permute-start
  8.9 0.2 convert_reduce_fusion
  9.2 0.7 all_to_all.9
  9.9 6.9 %all-to-all-start = ((s32[32,1,2]{2,1,0:T(1,128)}), s32[32,1,2]{2,1,0:T(1,128)S(1)}, u32[]{:S(2)}, u32[]{:S(2)}) async-start(s32[32,1,2]{2,1,0:T(1,128)} %bitcast), calls=%async_computation | async-start | bytes 32768 | tf_op jit(solution)/shard_map/all_to_all | solution.py:446
  16.9 1.3 collective-permute-start.2
  18.2 4.6 %collective-permute-start.1 = (f32[22,8,128]{2,1,0:T(8,128)S(1)}, f32[22,8,128]{2,1,0:T(8,128)S(1)}, u32[]{:S(2)}, u32[]{:S(2)}) collective-permute-start(f32[22,8,128]{2,1,0:T(8,128)S(1)} %pad_maximum_fusion), channel_id=1, source_target_pairs={{0,2},{2,4},{4,6},{6,8},{8,10},{10,12},{12,14},{14,16},{16,18},{18... | collective-permute-start | bytes 270344 | tf_op jit(solution)/shard_map/ppermute | solution.py:413
  22.8 0.8 collective-permute-done.2.refs_6_
  23.6 2.8 %collective-permute-done.1.refs_5_ = f32[22,8,128]{2,1,0:T(8,128)S(1)} collective-permute-done((f32[22,8,128]{2,1,0:T(8,128)S(1)}, f32[22,8,128]{2,1,0:T(8,128)S(1)}, u32[]{:S(2)}, u32[]{:S(2)}) %collective-permute-start.1) | collective-permute-done | bytes 90144 | tf_op jit(solution)/shard_map/ppermute | solution.py:413
  26.4 1.3 copy-done.1
  27.7 7.7 %step.1 = (f32[19,4,8,512]{3,2,1,0:T(8,128)S(1)}, f32[19,4,8,512]{3,2,1,0:T(8,128)S(1)}, f32[19,4,8,512]{3,2,1,0:T(8,128)S(1)}, f32[20,8,128]{2,1,0:T(8,128)S(1)...) custom-call(s32[2]{0:T(128)S(1)} %add_convert_fusion.refs_0_, ...), custom_call_target="tpu_custom_call" | custom-call | tf_op jit(solution)/shard_map/step/pallas_call | solution.py:464
  35.4 1.0 copy-done.2
  36.4 1.1 copy-done.4
  37.5 1.0 copy-done.6
  38.6 0.6 broadcast.45
  39.1 0.7 reduce.3
  39.9 0.1 eq.55
  40.0 1.3 collective-permute-start.5
  41.3 5.0 %collective-permute-start.4 = (f32[22,8,128]{2,1,0:T(8,128)S(1)}, f32[22,8,128]{2,1,0:T(8,128)S(1)}, u32[]{:S(2)}, u32[]{:S(2)}) collective-permute-start(f32[22,8,128]{2,1,0:T(8,128)S(1)} %pad_maximum_fusion.2), channel_id=1, source_target_pairs={{0,2},{2,4},{4,6},{6,8},{8,10},{10,12},{12,14},{14,16},{16,18},{18... | collective-permute-start | bytes 270344 | tf_op jit(solution)/shard_map/ppermute | solution.py:413
  46.3 0.2 select_reduce_fusion.refs_10_.slots
  46.5 1.1 collective-permute-done.5.refs_6_
  47.7 3.1 %collective-permute-done.4.refs_5_ = f32[22,8,128]{2,1,0:T(8,128)S(1)} collective-permute-done((f32[22,8,128]{2,1,0:T(8,128)S(1)}, f32[22,8,128]{2,1,0:T(8,128)S(1)}, u32[]{:S(2)}, u32[]{:S(2)}) %collective-permute-start.4) | collective-permute-done | bytes 90144 | tf_op jit(solution)/shard_map/ppermute | solution.py:413
  50.8 1.3 copy-done.3
  52.1 1.3 copy-done.5
  53.4 1.3 copy-done.7
  54.7 10.1 %last.1 = f32[64,80,128]{2,1,0:T(8,128)S(1)} custom-call(s32[2]{0:T(128)S(1)} %add_convert_fusion.refs_0_, s32[4,8,128]{2,1,0:T(8,128)S(1)} %broadcast_in_dim.45.level_ref.refs_1_, f32[19,4,8,512]{3,2,1,0:T(8,128)S(1)} %copy-done.3, f32[19,4,8,512]{3,2,1,0:T(8,128)S(1)} %copy-done.5, f32[19,4,8,512]{3,2,1,0:T(8,128)S(1)} %copy-done.7, ...), custom_call_target="tpu_custom_call" | custom-call | tf_op jit(solution)/shard_map/last/pallas_call | solution.py:473
  64.7 67.2 %all_to_all.14 = f32[32,160,128]{2,1,0:T(8,128)S(1)} all-to-all(f32[32,160,128]{2,1,0:T(8,128)S(1)} %bitcast.5), channel_id=1, replica_groups=mesh['blocks'=16,'cross'=2] {'blocks','cross'}, dimensions={0} | all-to-all | bytes 5242880 | tf_op jit(solution)/shard_map/all_to_all | solution.py:483
  131.9 3.1 %unpack.1 = f32[32,19,512]{2,1,0:T(8,128)S(1)} custom-call(s32[32]{0:T(128)S(1)} %select_reduce_fusion.refs_10_.slots, f32[64,80,128]{2,1,0:T(8,128)S(1)} %bitcast.6), custom_call_target="tpu_custom_call" | custom-call | tf_op jit(solution)/shard_map/unpack/pallas_call | solution.py:490
  135.0 1.8 %copy.13 = f32[32,19,512]{2,0,1:T(8,128)} copy(f32[32,19,512]{2,1,0:T(8,128)S(1)} %unpack.1) | data formatting | bytes 2490368 | tf_op jit(solution)/shard_map/unpack/pallas_call | solution.py:490
  (26 shorter events, 0.4 us)
Async XLA Ops:
  2.8 6.1 %copy-start.8 = (s32[32]{0:T(128)S(1)}, s32[32]{0:T(128)}, u32[]{:S(2)}) copy-start(s32[32]{0:T(128)} %param.5) | copy-start | bytes 388
  7.3 1.0 copy-start
  8.4 8.5 %collective-permute-start = (f32[16,8,128]{2,1,0:T(8,128)S(1)}, f32[16,8,128]{2,1,0:T(8,128)S(1)}, u32[]{:S(2)}, u32[]{:S(2)}) collective-permute-start(f32[16,8,128]{2,1,0:T(8,128)S(1)} %get-tuple-element.21), channel_id=1, source_target_pairs={{0,1},{1,0},{2,3},{3,2},{4,5},{5,4},{6,7},{7,6},{8,9},{9,8},{10,11... | collective-permute-start | bytes 196616 | tf_op jit(solution)/shard_map/ppermute | solution.py:408
  9.9 28.7 %all-to-all-start = ((s32[32,1,2]{2,1,0:T(1,128)}), s32[32,1,2]{2,1,0:T(1,128)S(1)}, u32[]{:S(2)}, u32[]{:S(2)}) async-start(s32[32,1,2]{2,1,0:T(1,128)} %bitcast), calls=%async_computation | async-start | bytes 32768 | tf_op jit(solution)/shard_map/all_to_all | solution.py:446
  16.9 6.7 %collective-permute-start.2 = (f32[22,8,128]{2,1,0:T(8,128)S(1)}, f32[22,8,128]{2,1,0:T(8,128)S(1)}, u32[]{:S(2)}, u32[]{:S(2)}) collective-permute-start(f32[22,8,128]{2,1,0:T(8,128)S(1)} %pad_maximum_fusion.1), channel_id=1, source_target_pairs={{2,0},{4,2},{6,4},{8,6},{10,8},{12,10},{14,12},{16,14},{18,16},{20... | collective-permute-start | bytes 270344 | tf_op jit(solution)/shard_map/ppermute | solution.py:413
  18.2 8.2 %collective-permute-start.1 = (f32[22,8,128]{2,1,0:T(8,128)S(1)}, f32[22,8,128]{2,1,0:T(8,128)S(1)}, u32[]{:S(2)}, u32[]{:S(2)}) collective-permute-start(f32[22,8,128]{2,1,0:T(8,128)S(1)} %pad_maximum_fusion), channel_id=1, source_target_pairs={{0,2},{2,4},{4,6},{6,8},{8,10},{10,12},{12,14},{14,16},{16,18},{18... | collective-permute-start | bytes 270344 | tf_op jit(solution)/shard_map/ppermute | solution.py:413
  26.4 1.3 copy-start.1
  35.4 1.0 copy-start.2
  36.4 1.1 copy-start.4
  37.5 1.0 copy-start.6
  38.5 1.4 %collective-permute-start.3 = (f32[16,8,128]{2,1,0:T(8,128)S(1)}, f32[16,8,128]{2,1,0:T(8,128)S(1)}, u32[]{:S(2)}, u32[]{:S(2)}) collective-permute-start(f32[16,8,128]{2,1,0:T(8,128)S(1)} %get-tuple-element.27), channel_id=1, source_target_pairs={{0,1},{1,0},{2,3},{3,2},{4,5},{5,4},{6,7},{7,6},{8,9},{9,8},{10,11... | collective-permute-start | bytes 196616 | tf_op jit(solution)/shard_map/ppermute | solution.py:408
  40.0 7.7 %collective-permute-start.5 = (f32[22,8,128]{2,1,0:T(8,128)S(1)}, f32[22,8,128]{2,1,0:T(8,128)S(1)}, u32[]{:S(2)}, u32[]{:S(2)}) collective-permute-start(f32[22,8,128]{2,1,0:T(8,128)S(1)} %pad_maximum_fusion.3), channel_id=1, source_target_pairs={{2,0},{4,2},{6,4},{8,6},{10,8},{12,10},{14,12},{16,14},{18,16},{20... | collective-permute-start | bytes 270344 | tf_op jit(solution)/shard_map/ppermute | solution.py:413
  41.3 9.5 %collective-permute-start.4 = (f32[22,8,128]{2,1,0:T(8,128)S(1)}, f32[22,8,128]{2,1,0:T(8,128)S(1)}, u32[]{:S(2)}, u32[]{:S(2)}) collective-permute-start(f32[22,8,128]{2,1,0:T(8,128)S(1)} %pad_maximum_fusion.2), channel_id=1, source_target_pairs={{0,2},{2,4},{4,6},{6,8},{8,10},{10,12},{12,14},{14,16},{16,18},{18... | collective-permute-start | bytes 270344 | tf_op jit(solution)/shard_map/ppermute | solution.py:413
  50.8 1.3 copy-start.3
  52.1 1.3 copy-start.5
  53.4 1.3 copy-start.7

commit v3 on v2

--- a/solution.py
+++ b/solution.py
@@ -223,26 +223,29 @@
     return jnp.where(fine, 1.0 / TAU_FINE, 1.0 / TAU_COARSE)
 
 
-def relax(masks, field, fine, row, tile, relaxed_ref, eq, neq):
+def relax(field, fine, row, tile, relaxed_ref, eq, neq):
     balance = equilibria(field)
     rate = rates(fine)
     send = jnp.where(fine, 1.0 / RESCALE, 1.0)
     for q in range(SPEEDS):
         relaxed = field[q] + rate * (balance[q] - field[q])
-        relaxed_ref[q, row, :, lanes_of(tile)] = relaxed
+        if relaxed_ref is not None:
+            relaxed_ref[q, row, :, lanes_of(tile)] = relaxed
         if q:
             eq[q, row, :, lanes_of(tile)] = balance[q]
             neq[q, row, :, lanes_of(tile)] = send * (relaxed - balance[q])
 
 
-def open_kernel(level_ref, field_ref, relaxed_ref, eq, neq, east, west, span):
+def open_kernel(level_ref, field_ref, moved_ref, east, west, span, eq, neq):
     masks = Masks()
 
     def row_step(row, carry):
         fine = level_ref[row] == 1
         for tile in range(TILES):
             field = [field_ref[pl.ds(row * 8, 8), q, lanes_of(tile)] for q in range(SPEEDS)]
-            relax(masks, field, fine, row, tile, relaxed_ref, eq, neq)
+            for q in range(SPEEDS):
+                moved_ref[q, row, :, lanes_of(tile)] = field[q]
+            relax(field, fine, row, tile, None, eq, neq)
         return carry
 
     lax.fori_loop(0, SPAN_PATCHES, row_step, 0)
@@ -250,15 +253,25 @@
 
 
 def step_kernel(final, *refs):
-    ends, level_ref, relaxed_ref, eq, neq, east, west, north, south = refs[:9]
+    ends, level_ref, field_ref, east, west, north, south = refs[:7]
     if final:
-        targets, _, moved_ref = refs[9:12]
-        span_eq, span_neq, side_eq, side_neq, ghost, fresh, again, rows_ref, sems = refs[12:]
+        targets, _, moved_ref = refs[7:10]
+        held, (rows_ref, sems) = refs[10:20], refs[20:]
     else:
-        relaxed_next, eq_next, neq_next, east_out, west_out, span_out = refs[9:15]
-        span_eq, span_neq, side_eq, side_neq, ghost, fresh, again = refs[15:]
+        moved_ref, east_out, west_out, span_out = refs[7:11]
+        held, (eq_next, neq_next) = refs[11:21], refs[21:]
+    relaxed_ref, eq, neq, span_eq, span_neq, side_eq, side_neq, ghost, fresh, again = held
     masks = Masks()
     take_halos(ends, span_eq, span_neq, side_eq, side_neq, east, west, north, south)
+
+    def collide_row(row, carry):
+        fine = level_ref[row] == 1
+        for tile in range(TILES):
+            field = [field_ref[q, row, :, lanes_of(tile)] for q in range(SPEEDS)]
+            relax(field, fine, row, tile, relaxed_ref, eq, neq)
+        return carry
+
+    lax.fori_loop(0, SPAN_PATCHES, collide_row, 0)
 
     def move_row(row, carry):
         fine = level_ref[row] == 1
@@ -318,14 +331,14 @@
                     start = row * (8 * ROWS) + (q * TILES + tile)
                     rows_ref[pl.ds(start, 8, stride=ROWS), :] = value
                 else:
-                    fresh[q, :, lanes_of(tile)] = value
+                    moved_ref[q, row, :, lanes_of(tile)] = value
         if final:
             for depth in range(8):
                 patch_copy(row * 8 + depth).start()
         else:
             for tile in range(TILES):
-                field = [fresh[q, :, lanes_of(tile)] for q in range(SPEEDS)]
-                relax(masks, field, fine, row, tile, relaxed_next, eq_next, neq_next)
+                field = [moved_ref[q, row, :, lanes_of(tile)] for q in range(SPEEDS)]
+                relax(field, fine, row, tile, None, eq_next, neq_next)
         return carry
 
     def patch_copy(patch):
@@ -347,7 +360,7 @@
         emit_halos(masks, eq_next, neq_next, east_out, west_out, span_out)
 
 
-def unpack_kernel(patches, slots, received, out_ref, rows_ref, sems):
+def unpack_kernel(patches, slots, received, out_ref, rows_ref, placed_ref, sems, out_sems):
     def patch_copy(patch):
         return pltpu.make_async_copy(
             received.at[slots[patch]],
@@ -355,6 +368,11 @@
             sems.at[patch],
         )
 
+    def out_copy(patch):
+        return pltpu.make_async_copy(
+            placed_ref.at[patch], out_ref.at[patch], out_sems.at[patch]
+        )
+
     def launch(patch, carry):
         patch_copy(patch).start()
         return carry
@@ -365,13 +383,19 @@
             count = min(8, SPEEDS - first)
             for tile in range(TILES):
                 start = patch * ROWS + (first * TILES + tile)
-                out_ref[patch, first : first + count, lanes_of(tile)] = rows_ref[
+                placed_ref[patch, first : first + count, lanes_of(tile)] = rows_ref[
                     pl.ds(start, count, stride=TILES), :
                 ]
+        out_copy(patch).start()
         return carry
 
     lax.fori_loop(0, patches, launch, 0)
+    def drain(patch, carry):
+        out_copy(patch).wait()
+        return carry
+
     lax.fori_loop(0, patches, place, 0)
+    lax.fori_loop(0, patches, drain, 0)
 
 
 def shape(*dims):
@@ -387,8 +411,6 @@
 ROW = (SPEEDS, DEPTH_PATCHES, CELLS)
 SPAN = (len(X_SPEEDS), DEPTH_PATCHES, CELLS)
 HANDED = (
-    shape(*FIELD),
-    shape(*FIELD),
     shape(*FIELD),
     shape(5 * SPAN_PATCHES, DEPTH_PATCHES, LANES),
     shape(5 * SPAN_PATCHES, DEPTH_PATCHES, LANES),
@@ -454,32 +476,34 @@
         open_kernel,
         out_shape=HANDED,
         in_specs=[VMEM, VMEM],
-        out_specs=[VMEM] * 6,
+        out_specs=[VMEM] * 4,
+        scratch_shapes=[scratch(FIELD), scratch(FIELD)],
         compiler_params=PARAMS,
         name="open",
     )(level_rows, f_home)
-    common = [scratch(SPAN), scratch(SPAN), scratch(SIDE), scratch(SIDE)]
+    common = [scratch(FIELD), scratch(FIELD), scratch(FIELD)]
+    common += [scratch(SPAN), scratch(SPAN), scratch(SIDE), scratch(SIDE)]
     common += [scratch(ROW), scratch(ROW), scratch(ROW)]
     for _ in range(STEPS - 1):
         outs = pl.pallas_call(
             functools.partial(step_kernel, False),
             out_shape=HANDED,
-            in_specs=[SMEM] + [VMEM] * 8,
-            out_specs=[VMEM] * 6,
-            scratch_shapes=common,
+            in_specs=[SMEM] + [VMEM] * 6,
+            out_specs=[VMEM] * 4,
+            scratch_shapes=common + [scratch(FIELD), scratch(FIELD)],
             compiler_params=PARAMS,
             name="step",
-        )(ends, level_rows, *outs[:3], *exchange(*outs[3:]))
+        )(ends, level_rows, outs[0], *exchange(*outs[1:]))
     packed = pl.pallas_call(
         functools.partial(step_kernel, True),
         out_shape=shape(devices * capacity, ROWS, LANES),
-        in_specs=[SMEM] + [VMEM] * 8 + [SMEM, SMEM],
+        in_specs=[SMEM] + [VMEM] * 6 + [SMEM, SMEM],
         out_specs=ANY,
         scratch_shapes=common
         + [scratch((patches * ROWS, LANES)), pltpu.SemaphoreType.DMA((patches,))],
         compiler_params=PARAMS,
         name="last",
-    )(ends, level_rows, *outs[:3], *exchange(*outs[3:]), targets, slots)
+    )(ends, level_rows, outs[0], *exchange(*outs[1:]), targets, slots)
     received = lax.all_to_all(
         packed.reshape(devices, capacity * ROWS, LANES),
         ("blocks", "cross"),
@@ -491,8 +515,13 @@
         functools.partial(unpack_kernel, patches),
         out_shape=shape(*f_home.shape),
         in_specs=[SMEM, ANY],
-        out_specs=VMEM,
-        scratch_shapes=[scratch((patches * ROWS, LANES)), pltpu.SemaphoreType.DMA((patches,))],
+        out_specs=pl.BlockSpec(memory_space=pltpu.HBM),
+        scratch_shapes=[
+            scratch((patches * ROWS, LANES)),
+            scratch(f_home.shape),
+            pltpu.SemaphoreType.DMA((patches,)),
+            pltpu.SemaphoreType.DMA((patches,)),
+        ],
         compiler_params=PARAMS,
         name="unpack",
     )(slots, received)

time: 137 us -> 132 us (0.964)
  local copies, waits for them, and re-layouts: 15.3 us -> 5.96 us
  Pallas kernels: 25.3 us -> 29.2 us
  waiting for transfers between devices: 7.87 us -> 10.2 us
  starting transfers between devices: 19.6 us -> 18.1 us
    unnamed x19 -> x3, local copies, waits for them, and re-layouts: 11.4 us -> 2.05 us
    pallas_call x1, Pallas kernels: 3.06 us -> 5.69 us  [body(): pl.pallas_call(functools.partial(unpack_kernel, patches), out_shape=shape...]
    ppermute x4, waiting for transfers between devices: 7.86 us -> 10.2 us  [send_flow(): return lax.ppermute(whole, 'blocks', pairs)]
    ppermute x4, starting transfers between devices: 12.2 us -> 10.5 us  [send_flow(): return lax.ppermute(whole, 'blocks', pairs)]
where the time goes in v3:
time: 132 us; the launch traced here: 131 us
  blocking collectives  66.5 us (50%)
  Pallas kernels  29.2 us (22%)
  starting transfers between devices  18.1 us (14%)
  waiting for transfers between devices  10.2 us (8%)
  local copies, waits for them, and re-layouts  5.96 us (5%)
    all_to_all x1, blocking collectives, body(): lax.all_to_all(packed.reshape(devices, capacity * ROWS, LANES), ('blocks'...  66.5 us
    pallas_call x1, Pallas kernels, body(): pl.pallas_call(functools.partial(step_kernel, True), out_shape=shape(devi...  10.7 us
    ppermute x4, starting transfers between devices, send_flow(): return lax.ppermute(whole, 'blocks', pairs)  10.5 us
    ppermute x4, waiting for transfers between devices, send_flow(): return lax.ppermute(whole, 'blocks', pairs)  10.2 us
    pallas_call x1, Pallas kernels, body(): pl.pallas_call(functools.partial(step_kernel, False), out_shape=HANDED, i...  8.26 us
    all_to_all x1, starting transfers between devices, body(): lax.all_to_all(table.reshape(devices, capacity), ('blocks', 'cross'), 0,...  6.95 us
    pallas_call x1, Pallas kernels, body(): pl.pallas_call(functools.partial(unpack_kernel, patches), out_shape=shape...  5.69 us
    pallas_call x1, Pallas kernels, body(): pl.pallas_call(open_kernel, out_shape=HANDED, in_specs=[VMEM, VMEM], out_...  4.53 us
  transfers between devices with their start and end apart: 7, of which 4 were waited for; matrix products, arithmetic and copies ran while one was open for 1% of the time, Pallas kernels for 6%

profile of v3, /device:TPU:0, one launch (start us, length us, event | category | flops | bytes accessed | tf_op | source)
XLA Modules:
  0.0 131.4 jit_solution(9221428171563635979)
XLA Ops:
  0.0 0.7 broadcast_in_dim.44
  0.7 2.0 %copy.12.field_ref = f32[32,19,512]{2,1,0:T(8,128)S(1)} copy(f32[32,19,512]{2,0,1:T(8,128)} %param.3) | data formatting | bytes 2490368 | tf_op args[0]
  2.8 0.1 broadcast_in_dim.45.level_ref.refs_1_
  2.9 4.5 %open.1 = (f32[19,4,8,512]{3,2,1,0:T(8,128)S(1)}, f32[20,8,128]{2,1,0:T(8,128)S(1)}, f32[20,8,128]{2,1,0:T(8,128)S(1)}, f32[16,8,128]{2,1,0:T(8,128)S(1)}) custom-call(s32[4,8,128]{2,1,0:T(8,128)S(1)} %broadcast_in_dim.45.level_ref.refs_1_, f32[32,19,512]{2,1,0:T(8,128)S(1)} %copy.12.field_ref), custom_call_target="tpu_custom_call" | custom-call | tf_op jit(solution)/shard_map/open/pallas_call | solution.py:475
  7.4 0.6 collective-permute-start
  8.0 0.0 copy-done
  8.0 0.2 convert_reduce_fusion
  8.2 0.1 select_reduce_fusion.1
  8.2 0.7 all_to_all.9
  9.0 6.9 %all-to-all-start = ((s32[32,1,2]{2,1,0:T(1,128)}), s32[32,1,2]{2,1,0:T(1,128)S(1)}, u32[]{:S(2)}, u32[]{:S(2)}) async-start(s32[32,1,2]{2,1,0:T(1,128)} %bitcast), calls=%async_computation | async-start | bytes 32768 | tf_op jit(solution)/shard_map/all_to_all | solution.py:468
  15.9 0.0 collective-permute-done.refs_5_.refs_6_
  16.0 3.7 %collective-permute-start.1 = (f32[22,8,128]{2,1,0:T(8,128)S(1)}, f32[22,8,128]{2,1,0:T(8,128)S(1)}, u32[]{:S(2)}, u32[]{:S(2)}) collective-permute-start(f32[22,8,128]{2,1,0:T(8,128)S(1)} %pad_maximum_fusion), channel_id=1, source_target_pairs={{0,2},{2,4},{4,6},{6,8},{8,10},{10,12},{12,14},{14,16},{16,18},{18... | collective-permute-start | bytes 270344 | tf_op jit(solution)/shard_map/ppermute | solution.py:435
  19.7 1.3 collective-permute-start.2
  21.0 0.1 add_convert_fusion.refs_0_
  21.1 0.8 collective-permute-done.1.refs_3_
  21.8 4.3 %collective-permute-done.2.refs_4_ = f32[22,8,128]{2,1,0:T(8,128)S(1)} collective-permute-done((f32[22,8,128]{2,1,0:T(8,128)S(1)}, f32[22,8,128]{2,1,0:T(8,128)S(1)}, u32[]{:S(2)}, u32[]{:S(2)}) %collective-permute-start.2) | collective-permute-done | bytes 90144 | tf_op jit(solution)/shard_map/ppermute | solution.py:435
  26.1 8.3 %step.1 = (f32[19,4,8,512]{3,2,1,0:T(8,128)S(1)}, f32[20,8,128]{2,1,0:T(8,128)S(1)}, f32[20,8,128]{2,1,0:T(8,128)S(1)}, f32[16,8,128]{2,1,0:T(8,128)S(1)}) custom-call(s32[2]{0:T(128)S(1)} %add_convert_fusion.refs_0_, s32[4,8,128]{2,1,0:T(8,128)S(1)} %broadcast_in_dim.45.level_ref.refs_1_, f32[19,4,8,512]{3,2,1,0:T(8,128)S(1)} %get-tuple-element.13.refs_2_, ...), custom_call_target="tpu_custom_call" | custom-call | tf_op jit(solution)/shard_map/step/pallas_call | solution.py:488
  34.4 0.1 collective-permute-start.3
  34.5 0.0 all-to-all-done
  34.5 0.5 broadcast.45
  35.0 0.7 reduce.3
  35.7 0.1 eq.55
  35.8 0.0 collective-permute-done.3.refs_5_.refs_6_
  35.8 4.3 %collective-permute-start.4 = (f32[22,8,128]{2,1,0:T(8,128)S(1)}, f32[22,8,128]{2,1,0:T(8,128)S(1)}, u32[]{:S(2)}, u32[]{:S(2)}) collective-permute-start(f32[22,8,128]{2,1,0:T(8,128)S(1)} %pad_maximum_fusion.2), channel_id=1, source_target_pairs={{0,2},{2,4},{4,6},{6,8},{8,10},{10,12},{12,14},{14,16},{16,18},{18... | collective-permute-start | bytes 270344 | tf_op jit(solution)/shard_map/ppermute | solution.py:435
  40.1 1.3 collective-permute-start.5
  41.4 0.2 select_reduce_fusion.refs_8_.slots
  41.6 1.0 collective-permute-done.4.refs_3_
  42.6 4.1 %collective-permute-done.5.refs_4_ = f32[22,8,128]{2,1,0:T(8,128)S(1)} collective-permute-done((f32[22,8,128]{2,1,0:T(8,128)S(1)}, f32[22,8,128]{2,1,0:T(8,128)S(1)}, u32[]{:S(2)}, u32[]{:S(2)}) %collective-permute-start.5) | collective-permute-done | bytes 90144 | tf_op jit(solution)/shard_map/ppermute | solution.py:435
  46.7 10.7 %last.1 = f32[64,80,128]{2,1,0:T(8,128)S(1)} custom-call(s32[2]{0:T(128)S(1)} %add_convert_fusion.refs_0_, s32[4,8,128]{2,1,0:T(8,128)S(1)} %broadcast_in_dim.45.level_ref.refs_1_, f32[19,4,8,512]{3,2,1,0:T(8,128)S(1)} %get-tuple-element.17.refs_2_, f32[22,8,128]{2,1,0:T(8,128)S(1)} %collective-permute-done.4.refs_3_, ...), custom_call_target="tpu_custom_call" | custom-call | tf_op jit(solution)/shard_map/last/pallas_call | solution.py:497
  57.4 66.5 %all_to_all.14 = f32[32,160,128]{2,1,0:T(8,128)S(1)} all-to-all(f32[32,160,128]{2,1,0:T(8,128)S(1)} %bitcast.5), channel_id=1, replica_groups=mesh['blocks'=16,'cross'=2] {'blocks','cross'}, dimensions={0} | all-to-all | bytes 5242880 | tf_op jit(solution)/shard_map/all_to_all | solution.py:507
  123.9 5.7 %unpack.1 = f32[32,19,512]{2,1,0:T(8,128)S(1)} custom-call(s32[32]{0:T(128)S(1)} %select_reduce_fusion.refs_8_.slots, f32[64,80,128]{2,1,0:T(8,128)S(1)} %bitcast.6), custom_call_target="tpu_custom_call" | custom-call | tf_op jit(solution)/shard_map/unpack/pallas_call | solution.py:514
  129.6 1.8 %copy.13 = f32[32,19,512]{2,0,1:T(8,128)} copy(f32[32,19,512]{2,1,0:T(8,128)S(1)} %unpack.1) | data formatting | bytes 2490368 | tf_op jit(solution)/shard_map/unpack/pallas_call | solution.py:514
  (10 shorter events, 0.1 us)
Async XLA Ops:
  0.7 7.2 %copy-start = (s32[32]{0:T(128)S(1)}, s32[32]{0:T(128)}, u32[]{:S(2)}) copy-start(s32[32]{0:T(128)} %param.5) | copy-start | bytes 388
  7.4 8.5 %collective-permute-start = (f32[16,8,128]{2,1,0:T(8,128)S(1)}, f32[16,8,128]{2,1,0:T(8,128)S(1)}, u32[]{:S(2)}, u32[]{:S(2)}) collective-permute-start(f32[16,8,128]{2,1,0:T(8,128)S(1)} %get-tuple-element.15), channel_id=1, source_target_pairs={{0,1},{1,0},{2,3},{3,2},{4,5},{5,4},{6,7},{7,6},{8,9},{9,8},{10,11... | collective-permute-start | bytes 196616 | tf_op jit(solution)/shard_map/ppermute | solution.py:430
  9.0 25.5 %all-to-all-start = ((s32[32,1,2]{2,1,0:T(1,128)}), s32[32,1,2]{2,1,0:T(1,128)S(1)}, u32[]{:S(2)}, u32[]{:S(2)}) async-start(s32[32,1,2]{2,1,0:T(1,128)} %bitcast), calls=%async_computation | async-start | bytes 32768 | tf_op jit(solution)/shard_map/all_to_all | solution.py:468
  16.0 5.8 %collective-permute-start.1 = (f32[22,8,128]{2,1,0:T(8,128)S(1)}, f32[22,8,128]{2,1,0:T(8,128)S(1)}, u32[]{:S(2)}, u32[]{:S(2)}) collective-permute-start(f32[22,8,128]{2,1,0:T(8,128)S(1)} %pad_maximum_fusion), channel_id=1, source_target_pairs={{0,2},{2,4},{4,6},{6,8},{8,10},{10,12},{12,14},{14,16},{16,18},{18... | collective-permute-start | bytes 270344 | tf_op jit(solution)/shard_map/ppermute | solution.py:435
  19.7 6.4 %collective-permute-start.2 = (f32[22,8,128]{2,1,0:T(8,128)S(1)}, f32[22,8,128]{2,1,0:T(8,128)S(1)}, u32[]{:S(2)}, u32[]{:S(2)}) collective-permute-start(f32[22,8,128]{2,1,0:T(8,128)S(1)} %pad_maximum_fusion.1), channel_id=1, source_target_pairs={{2,0},{4,2},{6,4},{8,6},{10,8},{12,10},{14,12},{16,14},{18,16},{20... | collective-permute-start | bytes 270344 | tf_op jit(solution)/shard_map/ppermute | solution.py:435
  34.4 1.4 %collective-permute-start.3 = (f32[16,8,128]{2,1,0:T(8,128)S(1)}, f32[16,8,128]{2,1,0:T(8,128)S(1)}, u32[]{:S(2)}, u32[]{:S(2)}) collective-permute-start(f32[16,8,128]{2,1,0:T(8,128)S(1)} %get-tuple-element.19), channel_id=1, source_target_pairs={{0,1},{1,0},{2,3},{3,2},{4,5},{5,4},{6,7},{7,6},{8,9},{9,8},{10,11... | collective-permute-start | bytes 196616 | tf_op jit(solution)/shard_map/ppermute | solution.py:430
  35.8 6.8 %collective-permute-start.4 = (f32[22,8,128]{2,1,0:T(8,128)S(1)}, f32[22,8,128]{2,1,0:T(8,128)S(1)}, u32[]{:S(2)}, u32[]{:S(2)}) collective-permute-start(f32[22,8,128]{2,1,0:T(8,128)S(1)} %pad_maximum_fusion.2), channel_id=1, source_target_pairs={{0,2},{2,4},{4,6},{6,8},{8,10},{10,12},{12,14},{14,16},{16,18},{18... | collective-permute-start | bytes 270344 | tf_op jit(solution)/shard_map/ppermute | solution.py:435
  40.1 6.6 %collective-permute-start.5 = (f32[22,8,128]{2,1,0:T(8,128)S(1)}, f32[22,8,128]{2,1,0:T(8,128)S(1)}, u32[]{:S(2)}, u32[]{:S(2)}) collective-permute-start(f32[22,8,128]{2,1,0:T(8,128)S(1)} %pad_maximum_fusion.3), channel_id=1, source_target_pairs={{2,0},{4,2},{6,4},{8,6},{10,8},{12,10},{14,12},{16,14},{18,16},{20... | collective-permute-start | bytes 270344 | tf_op jit(solution)/shard_map/ppermute | solution.py:435
